TPU v7x, 32 devices: a whole 2x2x4 slice. The times are simulated.
32 devices in a mesh: space: 8 (over y, x, core), mode: 4 (over z).
Axes of the slice: x: 2, y: 2, z: 4, core: 2. Of those that a mesh axis runs over, the one named last changes fastest.
Arguments:
- test_modes: float32 [32, 3, 8, 16, 256], P(None, None, None, 'space'), may hold values from -6 to 6
- modes: float32 [128, 3, 8, 16, 256], P('mode', None, None, 'space'), may hold values from -6 to 6
Outputs:
- triad: float32 [32, 128, 128], P('space', 'mode')
All inputs are finite; a program needn't handle non-finite values.
Results may differ from a plain program's by a relative error of at most 0.000071.
Values sent between devices are 32-bit elements; how exact they have to be, the bound alone decides.
No kernel may reach another device: no remote copies, remote signals or barrier semaphores. Data moves between devices by JAX's collectives and lax.ppermute only.
A program may use at most 64 MiB of HBM per device.

v0:
```python
import math

import jax
import jax.numpy as jnp
from jax import lax
from jax.sharding import PartitionSpec as P

MODES = 128
NX = 256
NZ = 8
BLOCK = 2048


def extended(value, sides, width):
    for axis, dim in sides:
        size, length = (lax.axis_size(axis), value.shape[dim])
        up = [(i, (i + 1) % size) for i in range(size)]
        down = [(j, i) for i, j in up]
        last = lax.slice_in_dim(value, length - width, length, axis=dim)
        leading = lax.slice_in_dim(value, 0, width, axis=dim)
        before = lax.ppermute(last, axis, up)
        after = lax.ppermute(leading, axis, down)
        value = jnp.concatenate([before, value, after], axis=dim)
    return value


def central_diff(field, along):
    ahead = jnp.roll(field, -1, along) - jnp.roll(field, 1, along)
    farther = jnp.roll(field, -2, along) - jnp.roll(field, 2, along)
    return (8.0 * ahead - farther) / 12.0


def per_device(test_modes, modes):
    local_count = modes.shape[0]
    test_count = test_modes.shape[0]
    row_count = modes.shape[3]
    padded = extended(modes, (("space", 3),), 2)
    ahead = padded[:, :, :, 3 : row_count + 3] - padded[:, :, :, 1 : row_count + 1]
    farther = padded[:, :, :, 4 : row_count + 4] - padded[:, :, :, 0:row_count]
    along_y = (8.0 * ahead - farther) / 12.0
    gradients = jnp.stack([central_diff(modes, 4), along_y, central_diff(modes, 2)], axis=2)
    gradients = gradients.reshape(local_count, 3, 3, -1)
    test_flat = test_modes.reshape(test_count, 3, -1)
    mode_flat = modes.reshape(local_count, 3, -1)
    cell_count = test_flat.shape[2]
    block_count = cell_count // BLOCK
    volume_scale = 1.0 / math.sqrt(NX * NZ * row_count * lax.axis_size("space"))

    def weigh(offset):
        test_block = lax.dynamic_slice_in_dim(test_flat, offset, BLOCK, 2)
        grad_block = lax.dynamic_slice_in_dim(gradients, offset, BLOCK, 3)
        weighted = test_block[:, 0, None, None, :] * grad_block[None, :, 0]
        weighted = weighted + test_block[:, 1, None, None, :] * grad_block[None, :, 1]
        weighted = weighted + test_block[:, 2, None, None, :] * grad_block[None, :, 2]
        return weighted

    def add_piece(running, weighted, piece_block):
        partial_value = jnp.einsum(
            "ikbc,jbc->ikj", weighted, piece_block, precision=lax.Precision.HIGHEST
        )
        return running + partial_value

    initial = jnp.zeros((test_count, local_count, MODES), jnp.float32)
    everything = lax.all_gather(mode_flat, "mode", axis=0, tiled=True)

    def one_block(index_block, running):
        offset = index_block * BLOCK
        weighted = weigh(offset)
        piece_block = lax.dynamic_slice_in_dim(everything, offset, BLOCK, 2)
        return add_piece(running, weighted, piece_block)

    partial_triad = lax.fori_loop(0, block_count, one_block, initial)
    partial_triad = partial_triad * volume_scale
    result = lax.psum_scatter(partial_triad, "space", scatter_dimension=0, tiled=True)
    return result


def solution(mesh):
    in_specs = (P(None, None, None, "space", None), P("mode", None, None, "space", None))
    out_specs = P("space", "mode", None)
    return jax.shard_map(
        per_device, mesh=mesh, in_specs=in_specs, out_specs=out_specs, check_vma=False
    )
```

profile of v0, /device:TPU:0, one launch (start us, length us, event | category | flops | bytes accessed | tf_op | source)
XLA Modules:
  0.0 227.1 jit_solution(10343335333044649658)
XLA Ops:
  6.5 2.1 copy.22
  8.6 2.4 %reshape.134 = f32[32,3,4096]{2,0,1:T(8,128)} reshape(f32[32,3,8,2,256]{4,3,2,0,1:T(2,128)S(1)} %copy.22) | data formatting | bytes 3145728 | tf_op jit(solution)/shard_map/reshape | solution.py:44
  11.1 1.3 copy-done
  12.5 3.4 %collective-permute-start = (f32[32,3,8,2,256]{4,3,2,1,0:T(2,128)S(1)}, f32[32,3,8,2,256]{4,3,2,1,0:T(2,128)}, u32[]{:S(2)}, u32[]{:S(2)}) collective-permute-start(f32[32,3,8,2,256]{4,3,2,1,0:T(2,128)S(1)} %copy-done), channel_id=1, source_target_pairs={{4,0},{8,4},{12,8},{16,12},{20,16},{24,20},{28,24},{0,28},{5,1},{9... | collective-permute-start | bytes 4718600 | tf_op jit(solution)/shard_map/ppermute | solution.py:22
  15.8 1.1 fusion.35
  16.9 1.2 copy.24
  18.1 1.7 copy.14
  19.9 1.0 copy.25
  20.9 1.7 copy.16
  22.6 1.1 slice_bitcast_fusion.8
  23.7 2.2 slice_bitcast_fusion
  25.9 2.2 slice_bitcast_fusion.2
  28.1 6.2 %fusion.30 = f32[32,3,1,8,2,256]{5,4,3,1,0,2:T(2,128)S(1)} fusion(f32[32,3,1,8,2,1]{5,4,3,1,0,2:T(2,128)S(1)} %copy-done.3, f32[32,3,1,8,2,255]{5,4,3,1,0,2:T(2,128)S(1)} %get-tuple-element.141, f32[32,3,1,8,2,255]{5,4,3,1,0,2:T(2,128)S(1)} %get-tuple-element.140, f32[32,3,1,8,2,1]{5,4,3,1,0,2:T(2,128)S(1)} %copy-done.4, ...), kind=kLoop, calls=%fused_computation.32 | loop fusion | flops 3538944 | bytes 7864320 | tf_op jit(solution)/shard_map/div | solution.py:30
  34.5 1.8 copy.17
  36.3 2.7 %div.14 = f32[32,3,1,4096]{3,0,2,1:T(8,128)S(1)} reshape(f32[32,3,1,8,2,256]{5,4,3,0,1,2:T(2,128)} %copy.17) | data formatting | bytes 3145728 | tf_op jit(solution)/shard_map/div | solution.py:30
  40.9 2.6 %fusion.33 = f32[32,3,1,8,2,256]{5,4,3,1,0,2:T(2,128)S(1)} fusion(f32[32,3,1,1,2,256]{5,4,3,1,0,2:T(2,128)S(1)} %get-tuple-element.147, f32[32,3,1,7,2,256]{5,4,3,1,0,2:T(2,128)S(1)} %get-tuple-element.149, f32[32,3,1,7,2,256]{5,4,3,1,0,2:T(2,128)S(1)} %get-tuple-element.148, f32[32,3,1,1,2,256]{5,4,3,1,0,2:T(2,128)S(1)} %get-tuple-element.146, ...), kind=kLoop, calls=%fused_computation.37 | loop fusion | flops 3538944 | bytes 7864320 | tf_op jit(solution)/shard_map/div | solution.py:30
  43.6 1.7 copy.21
  45.3 3.3 %div.17 = f32[32,3,1,4096]{3,0,2,1:T(8,128)} reshape(f32[32,3,1,8,2,256]{5,4,3,0,1,2:T(2,128)} %copy.21) | data formatting | bytes 3145728 | tf_op jit(solution)/shard_map/div | solution.py:30
  48.6 3.3 %copy.12 = f32[32,3,8,2,256]{4,3,2,0,1:T(2,128)} copy(f32[32,3,8,2,256]{4,3,2,1,0:T(2,128)} %param.4) | data formatting | bytes 3145728 | tf_op args[0]
  51.9 3.3 %reshape.133 = f32[32,3,4096]{2,0,1:T(8,128)} reshape(f32[32,3,8,2,256]{4,3,2,0,1:T(2,128)} %copy.12) | data formatting | bytes 3145728 | tf_op jit(solution)/shard_map/reshape | solution.py:43
  55.2 6.9 %fusion.34 = f32[32,3,8,2,256]{4,3,2,1,0:T(2,128)S(1)} fusion(f32[32,3,8,2,256]{4,3,2,1,0:T(2,128)} %collective-permute-done, f32[32,3,8,2,256]{4,3,2,1,0:T(2,128)} %collective-permute-done.1, f32[32,3,8,2,256]{4,3,2,1,0:T(2,128)S(1)} %copy-done), kind=kLoop, calls=%fused_computation.43 | loop fusion | flops 2752512 | bytes 6291456 | tf_op jit(solution)/shard_map/div | solution.py:40
  62.1 1.7 copy.18
  63.8 3.5 %stack.8 = f32[32,3,1,4096]{3,0,2,1:T(8,128)} reshape(f32[32,3,8,2,256]{4,3,2,0,1:T(2,128)} %copy.18) | data formatting | bytes 3145728 | tf_op jit(solution)/shard_map/stack | solution.py:41
  67.3 4.0 %pad_maximum_fusion = f32[32,3,3,4096]{3,0,2,1:T(8,128)} fusion(f32[32,3,1,4096]{3,0,2,1:T(8,128)S(1)} %copy-done.2, f32[32,3,1,4096]{3,0,2,1:T(8,128)} %stack.8, f32[32,3,1,4096]{3,0,2,1:T(8,128)S(1)} %div.14), kind=kLoop, calls=%fused_computation.23 | loop fusion | flops 2359296 | bytes 9437184 | tf_op jit(solution)/shard_map/stack | solution.py:41
  71.3 58.0 %all-gather.2.cloned.1.call-done = f32[128,3,4096]{2,0,1:T(8,128)} async-done(((f32[32,3,4096]{2,0,1:T(8,128)}), f32[128,3,4096]{2,0,1:T(8,128)}) %all-gather.2.cloned.1.call-update) | async-done | bytes 6291472 | tf_op jit(solution)/shard_map/all_gather | solution.py:64
  129.3 56.1 %while.14 = (s32[]{:T(128)}, f32[32,32,128]{2,1,0:T(8,128)}, f32[32,3,4096]{2,0,1:T(8,128)}, f32[32,3,3,4096]{3,0,2,1:T(8,128)}, f32[128,3,4096]{2,0,1:T(8,128)}...) while((s32[]{:T(128)}, f32[32,32,128]{2,1,0:T(8,128)}, ...), condition=%wide.region_1.2_spmd.clone, body=%wide.region_0.1_spmd.clone.sunk | while | flops 9695395840 | bytes 19923188 | solution.py:72
  129.6 1.9 dynamic-slice_bitcast_fusion.8
  131.7 25.7 %fusion.41 = f32[32,32,128]{2,1,0:T(8,128)} fusion(f32[128,3,4096]{2,0,1:T(8,128)} %get-tuple-element.219, s32[]{:T(128)S(6)} %select_n.11, f32[32,3,2048]{2,0,1:T(8,128)S(1)} %get-tuple-element.187, f32[32,2048]{1,0:T(8,128)S(1)} %get-tuple-element.188, f32[32,3,2048]{2,0,1:T(8,128)S(1)} %get-tuple-element.189, ...), kind=kOutput, calls=%fused_computation.15.clone.1 | convolution fusion | flops 9695395840 | bytes 7340037 | tf_op jit(solution)/shard_map/while/body/eval_jaxpr/ikbc,jbc->ikj/dot_general | solution.py:58
  157.5 1.9 dynamic-slice_bitcast_fusion.8
  159.6 25.8 %fusion.41 = f32[32,32,128]{2,1,0:T(8,128)} fusion(f32[128,3,4096]{2,0,1:T(8,128)} %get-tuple-element.219, s32[]{:T(128)S(6)} %select_n.11, f32[32,3,2048]{2,0,1:T(8,128)S(1)} %get-tuple-element.187, f32[32,2048]{1,0:T(8,128)S(1)} %get-tuple-element.188, f32[32,3,2048]{2,0,1:T(8,128)S(1)} %get-tuple-element.189, ...), kind=kOutput, calls=%fused_computation.15.clone.1 | convolution fusion | flops 9695395840 | bytes 7340037 | tf_op jit(solution)/shard_map/while/body/eval_jaxpr/ikbc,jbc->ikj/dot_general | solution.py:58
  185.4 1.9 broadcast_multiply_fusion
  187.4 32.5 %reduce-scatter.2.cloned.1.call-done = f32[4,32,128]{2,1,0:T(8,128)} async-done(((f32[32,32,128]{2,1,0:T(8,128)}), f32[4,32,128]{2,1,0:T(8,128)}) %reduce-scatter.2.cloned.1.call-update) | async-done | bytes 65552 | tf_op jit(solution)/shard_map/reduce_scatter | solution.py:74
  (25 shorter events, 2.7 us)
Async XLA Ops:
  6.5 122.8 %all-gather.2.cloned.1.call-start = ((), (), s32[]{:S(2)}) async-start(), calls=%async_computation.1 | async-start | bytes 7864320 | tf_op jit(solution)/shard_map/all_gather | solution.py:64
  11.1 1.4 copy-start
  11.1 208.7 %reduce-scatter.2.cloned.1.call-start = ((), (), s32[]{:S(2)}) async-start(), calls=%async_computation.2 | async-start | bytes 589824 | tf_op jit(solution)/shard_map/reduce_scatter | solution.py:74
  12.5 42.8 %collective-permute-start = (f32[32,3,8,2,256]{4,3,2,1,0:T(2,128)S(1)}, f32[32,3,8,2,256]{4,3,2,1,0:T(2,128)}, u32[]{:S(2)}, u32[]{:S(2)}) collective-permute-start(f32[32,3,8,2,256]{4,3,2,1,0:T(2,128)S(1)} %copy-done), channel_id=1, source_target_pairs={{4,0},{8,4},{12,8},{16,12},{20,16},{24,20},{28,24},{0,28},{5,1},{9... | collective-permute-start | bytes 4718600 | tf_op jit(solution)/shard_map/ppermute | solution.py:22
  15.8 39.4 %collective-permute-start.1 = (f32[32,3,8,2,256]{4,3,2,1,0:T(2,128)S(1)}, f32[32,3,8,2,256]{4,3,2,1,0:T(2,128)}, u32[]{:S(2)}, u32[]{:S(2)}) collective-permute-start(f32[32,3,8,2,256]{4,3,2,1,0:T(2,128)S(1)} %copy-done), channel_id=1, source_target_pairs={{0,4},{4,8},{8,12},{12,16},{16,20},{20,24},{24,28},{28,0},{1,5},{5... | collective-permute-start | bytes 4718600 | tf_op jit(solution)/shard_map/ppermute | solution.py:21
  25.8 2.2 copy-start.3
  25.9 2.2 copy-start.4
  63.8 3.5 %copy-start.2 = (f32[32,3,1,4096]{3,0,2,1:T(8,128)S(1)}, f32[32,3,1,4096]{3,0,2,1:T(8,128)}, u32[]{:S(2)}) copy-start(f32[32,3,1,4096]{3,0,2,1:T(8,128)} %div.17) | copy-start | bytes 4718596
  129.5 2.1 copy-start.1
  157.4 2.1 copy-start.1
Sparse Core Ops, SparseCore 0:
  11.2 118.0 all-gather.1
  187.5 32.2 reduce-scatter.1
where the time goes:
time: 230 us; the launch traced here: 227 us
  waiting for transfers between devices  90.5 us (39%)
  matrix products  51.5 us (22%)
  local copies, waits for them, and re-layouts  45.7 us (20%)
  other arithmetic  21.6 us (9%)
  between operations  14 us (6%)
  starting transfers between devices  3.41 us (1%)
    all_gather x1, waiting for transfers between devices, per_device(): everything = lax.all_gather(mode_flat, 'mode', axis=0, tiled=True)  58 us
    dot_general x2, matrix products, add_piece(): jnp.einsum('ikbc,jbc->ikj', weighted, piece_block, precision=lax.Precisio...  51.5 us
    reduce_scatter x1, waiting for transfers between devices, per_device(): lax.psum_scatter(partial_triad, 'space', scatter_dimension=0, tiled=True)  32.5 us
    div x4, local copies, waits for them, and re-layouts, central_diff(): return (8.0 * ahead - farther) / 12.0  9.66 us
    unnamed x12, local copies, waits for them, and re-layouts  8.91 us
    div x2, other arithmetic, central_diff(): return (8.0 * ahead - farther) / 12.0  8.86 us
    div x1, other arithmetic, per_device(): along_y = (8.0 * ahead - farther) / 12.0  6.88 us
    concatenate x5, local copies, waits for them, and re-layouts, central_diff(): ahead = jnp.roll(field, -1, along) - jnp.roll(field, 1, along)  6.51 us
  transfers between devices with their start and end apart: 4, of which 2 were waited for; matrix products, arithmetic and copies ran while one was open for 24% of the time, Pallas kernels for 0%

commit v1 on v0

v1 whole, which is shorter than its diff:
```python
import math
from functools import partial

import jax
import jax.numpy as jnp
from jax import lax
from jax.experimental import pallas as pl
from jax.experimental.pallas import tpu as pltpu
from jax.sharding import PartitionSpec as P

LANES = 128
PITCH_PAD = 8


def flat_rows(field):
    count, comps, nz, rows, nx = field.shape
    tiles = nx // LANES
    split = field.reshape(count, comps, nz, rows, tiles, LANES)
    return split.transpose(0, 1, 2, 4, 3, 5).reshape(count, comps * nz * tiles * rows, LANES)


def lane_ids(count):
    return lax.broadcasted_iota(jnp.int32, (count, LANES), 1)


def chunk_kernel(dims, shifts, halos, me_ref, src_ref, *refs):
    count, nz, rows, nx, chunk, parts = dims
    tiles = nx // LANES
    outs, scratch, sem = refs[:-2], refs[-2], refs[-1]
    depth = 3 * nz * tiles * rows
    pitch = depth + PITCH_PAD
    copy = pltpu.make_async_copy(src_ref, scratch.reshape(count, pitch, LANES).at[:, pl.ds(0, depth), :], sem)
    copy.start()
    copy.wait()
    lane = lane_ids(count)

    def load(a, z, tile, y):
        return scratch[pl.ds(((a * nz + z) * tiles + tile) * rows + y, count, stride=pitch), :]

    def moved(value, amount):
        return pltpu.roll(value, lax.rem(amount + 2 * LANES, LANES), 1)

    for index, shift in enumerate(shifts):
        part = lax.rem(me_ref[0] + shift, parts)
        start = part * chunk
        left = lax.rem(start + nx - 2, nx)
        right = lax.rem(start + chunk, nx)
        field_out = outs[index]
        for a in range(3):
            packed = jnp.zeros((count, LANES), jnp.float32)
            for z in range(nz):
                value = jnp.zeros((count, LANES), jnp.float32)
                for y in range(rows):
                    row = moved(load(a, z, start // LANES, y), y * chunk - lax.rem(start, LANES))
                    mine = (lane >= y * chunk) & (lane < (y + 1) * chunk)
                    value = jnp.where(mine, row, value)
                    if halos:
                        at = y * chunk + 2 * z
                        low = moved(load(a, z, left // LANES, y), at - lax.rem(left, LANES))
                        packed = jnp.where((lane >= at) & (lane < at + 2), low, packed)
                        at = (y + 1) * chunk - 2 - 2 * z
                        high = moved(load(a, z, right // LANES, y), at - lax.rem(right, LANES))
                        packed = jnp.where((lane >= at) & (lane < at + 2), high, packed)
                field_out[z, a] = value
            if halos:
                field_out[nz, a] = packed


def chunks(field, me, parts, shifts, halos):
    count, comps, nz, rows, nx = field.shape
    chunk = nx // parts
    flat = flat_rows(field)
    dims = (count, nz, rows, nx, chunk, parts)
    shape = (nz + 1 if halos else nz, comps, count, LANES)
    return pl.pallas_call(
        partial(chunk_kernel, dims, shifts, halos),
        out_shape=[jax.ShapeDtypeStruct(shape, jnp.float32) for _ in shifts],
        in_specs=[pl.BlockSpec(memory_space=pltpu.SMEM), pl.BlockSpec(memory_space=pl.ANY)],
        scratch_shapes=[
            pltpu.VMEM((count * (flat.shape[1] + PITCH_PAD), LANES), jnp.float32),
            pltpu.SemaphoreType.DMA,
        ],
        name="chunks",
    )(me, flat)


def split_pair(value):
    high = value.astype(jnp.bfloat16)
    return high, (value - high.astype(jnp.float32)).astype(jnp.bfloat16)


def put_right(right_ref, unit, z, at, total, value):
    high, low = split_pair(value)
    count = value.shape[0]
    right_ref[unit, pl.ds(at, count), pl.ds(z * LANES, LANES)] = high
    right_ref[unit, pl.ds(total + at, count), pl.ds(z * LANES, LANES)] = low


def contract(units, nz, group, total, test_refs, grad_ref, right_ref, high_ref, low_ref):
    first = pl.program_id(0) * group
    for unit in range(units):
        for z in range(nz):
            tests = [[test_refs[unit][z, a, pl.ds(first + i, 1), :] for a in range(3)] for i in range(group)]
            grads = [grad_ref[(unit * 3 + a) * nz + z] for a in range(3)]
            for i in range(group):
                weighted = tests[i][0] * grads[0] + tests[i][1] * grads[1] + tests[i][2] * grads[2]
                high, low = split_pair(weighted)
                where = (pl.ds(i * total, total), pl.ds((unit * nz + z) * LANES, LANES))
                high_ref[where] = high
                low_ref[where] = low
    result = None
    for unit in range(units):
        span = pl.ds(unit * nz * LANES, nz * LANES)
        dims = (((1,), (1,)), ((), ()))
        both = lax.dot_general(high_ref[:, span], right_ref[unit], dims, preferred_element_type=jnp.float32)
        low = lax.dot_general(low_ref[:, span], right_ref[unit, :total], dims, preferred_element_type=jnp.float32)
        part = both[:, :total] + both[:, total:] + low
        result = part if result is None else result + part
    return result


def xz_kernel(dims, me_ref, test_ref, *refs):
    parts, count, nz, chunk, group = dims
    total = parts * count
    fields, (out_ref, grad_ref, right_ref, high_ref, low_ref) = refs[:parts], refs[parts:]

    @pl.when(pl.program_id(0) == 0)
    def _():
        lane = lane_ids(count)
        place = lax.rem(lane, chunk)
        for shift in range(parts):
            field = fields[shift]
            at = pl.multiple_of(lax.rem(me_ref[0] + parts - shift, parts) * count, count)

            def one_comp(a, carry):
                packed = field[nz, a]
                for z in range(nz):
                    value = field[z, a]
                    edge = jnp.where(place < 2, pltpu.roll(packed, (LANES - 2 * z) % LANES, 1), pltpu.roll(packed, 2 * z, 1))
                    up = jnp.where(place == chunk - 1, pltpu.roll(edge, 1, 1), pltpu.roll(value, LANES - 1, 1))
                    down = jnp.where(place == 0, pltpu.roll(edge, LANES - 1, 1), pltpu.roll(value, 1, 1))
                    up2 = jnp.where(place >= chunk - 2, edge, pltpu.roll(value, LANES - 2, 1))
                    down2 = jnp.where(place < 2, edge, pltpu.roll(value, 2, 1))
                    grad_ref[a * nz + z, pl.ds(at, count), :] = 8.0 * (up - down) - (up2 - down2)
                    ahead = field[(z + 1) % nz, a] - field[(z - 1) % nz, a]
                    farther = field[(z + 2) % nz, a] - field[(z - 2) % nz, a]
                    grad_ref[(3 + a) * nz + z, pl.ds(at, count), :] = 8.0 * ahead - farther
                return carry

            lax.fori_loop(0, 3, one_comp, 0)
            for z in range(nz):
                put_right(right_ref, 0, z, at, total, field[z, 0])
                put_right(right_ref, 1, z, at, total, field[z, 2])

    out_ref[...] = contract(2, nz, group, total, (test_ref, test_ref), grad_ref, right_ref, high_ref, low_ref)


def y_kernel(dims, me_ref, test_ref, next_test_ref, run_ref, *refs):
    parts, count, nz, chunk, group, scale = dims
    total = parts * count
    fields, nexts = refs[:parts], refs[parts : 2 * parts]
    out_ref, grad_ref, right_ref, high_ref, low_ref = refs[2 * parts :]

    @pl.when(pl.program_id(0) == 0)
    def _():
        lane = lane_ids(count)
        first = lane < chunk

        def swapped(value):
            if 2 * chunk == LANES:
                return pltpu.roll(value, chunk, 1)
            return jnp.where(first, pltpu.roll(value, LANES - chunk, 1), pltpu.roll(value, chunk, 1))

        for shift in range(parts):
            field, following = fields[shift], nexts[shift]
            at = pl.multiple_of(lax.rem(me_ref[0] + parts - shift, parts) * count, count)

            def one_comp(a, carry):
                for z in range(nz):
                    own, ahead = field[z, a], following[z, a]
                    turned = 8.0 * swapped(own)
                    mine = jnp.where(first, turned, 8.0 * swapped(ahead) - turned) - ahead
                    theirs = own - jnp.where(first, turned, 0.0)
                    grad_ref[a * nz + z, pl.ds(at, count), :] = mine
                    grad_ref[(3 + a) * nz + z, pl.ds(at, count), :] = theirs
                return carry

            lax.fori_loop(0, 3, one_comp, 0)
            for z in range(nz):
                put_right(right_ref, 0, z, at, total, field[z, 1])
                put_right(right_ref, 1, z, at, total, following[z, 1])

    part = contract(2, nz, group, total, (test_ref, next_test_ref), grad_ref, right_ref, high_ref, low_ref)
    out_ref[...] = (run_ref[...] + part) * scale


def part_call(kernel, name, me, whole, running, parts, count, nz, tests, group):
    total = parts * count
    keep = lambda value: pl.BlockSpec(value.shape, lambda g, nd=value.ndim: (0,) * nd, pipeline_mode=pl.Buffered(1))
    rows = pl.BlockSpec((group * total, total), lambda g: (g, 0))
    return pl.pallas_call(
        kernel,
        grid=(tests // group,),
        out_shape=jax.ShapeDtypeStruct((tests * total, total), jnp.float32),
        in_specs=[pl.BlockSpec(memory_space=pltpu.SMEM)]
        + [rows if value is running else keep(value) for value in whole],
        out_specs=rows,
        scratch_shapes=[
            pltpu.VMEM((6 * nz, total, LANES), jnp.float32),
            pltpu.VMEM((2, 2 * total, nz * LANES), jnp.bfloat16),
            pltpu.VMEM((group * total, 2 * nz * LANES), jnp.bfloat16),
            pltpu.VMEM((group * total, 2 * nz * LANES), jnp.bfloat16),
        ],
        compiler_params=pltpu.CompilerParams(dimension_semantics=("arbitrary",)),
        cost_estimate=pl.CostEstimate(flops=2 * 6 * nz * LANES * tests * total * total, transcendentals=0, bytes_accessed=8 * tests * total * total),
        name=name,
    )(me, *whole)


def shifted(value, axis, shift):
    size = lax.axis_size(axis)
    return lax.ppermute(value, axis, [(i, (i + shift) % size) for i in range(size)])


def scattered(value, axis, dim):
    size, me = lax.axis_size(axis), lax.axis_index(axis)
    length = value.shape[dim] // size
    total = lax.dynamic_slice_in_dim(value, me * length, length, dim)
    for shift in range(1, size):
        block = lax.dynamic_slice_in_dim(value, lax.rem(me + shift, size) * length, length, dim)
        total = total + shifted(block, axis, shift)
    return total


def per_device(test_modes, modes):
    count, comps, nz, rows, nx = modes.shape
    tests = test_modes.shape[0]
    parts = lax.axis_size("mode")
    total = parts * count
    chunk = nx // parts
    assert rows == 2 and rows * chunk <= LANES
    group = 4
    me = lax.axis_index("mode").astype(jnp.int32).reshape(1)
    scale = 1.0 / (12.0 * math.sqrt(nx * nz * rows * lax.axis_size("space")))

    sends = chunks(modes, me, parts, tuple(range(parts)), True)
    test = chunks(test_modes, me, parts, (0,), False)[0]
    next_test = shifted(test, "space", -1)
    fields = [sends[0]] + [shifted(sends[shift], "mode", shift) for shift in range(1, parts)]
    nexts = [shifted(field[:nz], "space", -1) for field in fields]

    running = part_call(
        partial(xz_kernel, (parts, count, nz, chunk, group)), "xz_part", me, [test] + fields, None,
        parts, count, nz, tests, group)
    partial_triad = part_call(
        partial(y_kernel, (parts, count, nz, chunk, group, scale)), "y_part", me,
        [test, next_test, running] + fields + nexts, running, parts, count, nz, tests, group)

    in_plane = scattered(partial_triad.reshape(tests, total, total), "space", 0)
    return scattered(in_plane, "mode", 1)


def solution(mesh):
    in_specs = (P(None, None, None, "space", None), P("mode", None, None, "space", None))
    return jax.shard_map(
        per_device, mesh=mesh, in_specs=in_specs, out_specs=P("space", "mode", None), check_vma=False
    )
```

time: 230 us -> 145 us (0.63); the launches traced: 227 us -> 145 us
  Pallas kernels: 0 us -> 61.7 us
  matrix products: 51.5 us -> 0 us
  local copies, waits for them, and re-layouts: 45.7 us -> 2.49 us
  waiting for transfers between devices: 90.5 us -> 49.6 us
  starting transfers between devices: 3.41 us -> 29 us
  other arithmetic: 21.6 us -> 1.7 us
  between operations: 14 us -> 0.12 us
    pallas_call x0 -> x4, Pallas kernels: none -> 61.7 us  [the longest x2 54.2 us: part_call(): pl.pallas_call(kernel, grid=(tests // group,), out_shape=jax.ShapeDtypeSt...]
    all_gather x1 -> x0, waiting for transfers between devices: 58 us -> none  [per_device(): everything = lax.all_gather(mode_flat, 'mode', axis=0, tiled=True)]
    dot_general x2 -> x0, matrix products: 51.5 us -> none  [add_piece(): jnp.einsum('ikbc,jbc->ikj', weighted, piece_block, precision=lax.Precisio...]
    ppermute x2 -> x18, waiting for transfers between devices: 0.01 us -> 49.6 us  [shifted(): lax.ppermute(value, axis, [(i, (i + shift) % size) for i in range(size)])]
    reduce_scatter x1 -> x0, waiting for transfers between devices: 32.5 us -> none  [per_device(): lax.psum_scatter(partial_triad, 'space', scatter_dimension=0, tiled=True)]
    ppermute x2 -> x18, starting transfers between devices: 3.36 us -> 29 us  [shifted(): lax.ppermute(value, axis, [(i, (i + shift) % size) for i in range(size)])]
    div x3 -> x0, other arithmetic: 15.7 us -> none  [the longest x2 8.86 us: central_diff(): return (8.0 * ahead - farther) / 12.0]
    div x5 -> x0, local copies, waits for them, and re-layouts: 11.4 us -> none  [the longest x4 9.66 us: central_diff(): return (8.0 * ahead - farther) / 12.0]
  transfers between devices with their start and end apart: 4 -> 18, of which waited for: 2 -> 10; matrix products, arithmetic and copies ran while one was open for 24% -> 0% of each run, Pallas kernels for 0% -> 22%
where the time goes in v1:
time: 145 us
  Pallas kernels  61.7 us (43%)
  waiting for transfers between devices  49.6 us (34%)
  starting transfers between devices  29 us (20%)
  local copies, waits for them, and re-layouts  2.49 us (2%)
  other arithmetic  1.7 us (1%)
    pallas_call x2, Pallas kernels, part_call(): pl.pallas_call(kernel, grid=(tests // group,), out_shape=jax.ShapeDtypeSt...  54.2 us
    ppermute x18, waiting for transfers between devices, shifted(): lax.ppermute(value, axis, [(i, (i + shift) % size) for i in range(size)])  49.6 us
    ppermute x18, starting transfers between devices, shifted(): lax.ppermute(value, axis, [(i, (i + shift) % size) for i in range(size)])  29 us
    pallas_call x2, Pallas kernels, chunks(): pl.pallas_call(partial(chunk_kernel, dims, shifts, halos), out_shape=[jax...  7.57 us
  transfers between devices with their start and end apart: 18, of which 10 were waited for; matrix products, arithmetic and copies ran while one was open for 0% of the time, Pallas kernels for 22%

profile of v1, /device:TPU:0, one launch (start us, length us, event | category | flops | bytes accessed | tf_op | source)
XLA Modules:
  0.0 144.7 jit_solution(15893686887259761981)
XLA Ops:
  0.0 5.1 %chunks.3 = (f32[9,3,32,128]{3,2,1,0:T(8,128)}, f32[9,3,32,128]{3,2,1,0:T(8,128)}, f32[9,3,32,128]{3,2,1,0:T(8,128)}, f32[9,3,32,128]{3,2,1,0:T(8,128)}) custom-call(s32[1]{0:T(128)} %bitcast.me_ref, f32[32,96,128]{2,1,0:T(8,128)} %bitcast.14), custom_call_target="tpu_custom_call" | custom-call | tf_op jit(solution)/shard_map/chunks/pallas_call | solution.py:75
  5.2 3.1 %collective-permute-start.1 = (f32[9,3,32,128]{3,2,1,0:T(8,128)}, f32[9,3,32,128]{3,2,1,0:T(8,128)S(1)}, u32[]{:S(2)}, u32[]{:S(2)}) collective-permute-start(f32[9,3,32,128]{3,2,1,0:T(8,128)} %get-tuple-element.10), channel_id=1, source_target_pairs={{0,1},{1,2},{2,3},{3,0},{4,5},{5,6},{6,7},{7,4},{8,9},{9,10},{10,1... | collective-permute-start | bytes 1327112 | tf_op jit(solution)/shard_map/ppermute | solution.py:222
  8.3 2.6 %collective-permute-start.2 = (f32[9,3,32,128]{3,2,1,0:T(8,128)}, f32[9,3,32,128]{3,2,1,0:T(8,128)S(1)}, u32[]{:S(2)}, u32[]{:S(2)}) collective-permute-start(f32[9,3,32,128]{3,2,1,0:T(8,128)} %get-tuple-element.11), channel_id=1, source_target_pairs={{0,2},{1,3},{2,0},{3,1},{4,6},{5,7},{6,4},{7,5},{8,10},{9,11},{10,... | collective-permute-start | bytes 1327112 | tf_op jit(solution)/shard_map/ppermute | solution.py:222
  10.9 1.3 collective-permute-start.3
  12.2 2.4 %chunks.2.test_ref = f32[8,3,32,128]{3,2,1,0:T(8,128)} custom-call(s32[1]{0:T(128)} %bitcast.me_ref, f32[32,96,128]{2,1,0:T(8,128)} %bitcast.15), custom_call_target="tpu_custom_call" | custom-call | tf_op jit(solution)/shard_map/chunks/pallas_call | solution.py:75
  14.6 1.1 collective-permute-start
  15.8 1.6 %collective-permute-start.4 = (f32[8,3,32,128]{3,2,1,0:T(8,128)S(1)}, f32[8,3,32,128]{3,2,1,0:T(8,128)S(1)}, u32[]{:S(2)}, u32[]{:S(2)}) collective-permute-start(f32[8,3,32,128]{3,2,1,0:T(8,128)S(1)} %slice.12), channel_id=1, source_target_pairs={{0,28},{4,0},{8,4},{12,8},{16,12},{20,16},{24,20},{28,24},{1,29},{... | collective-permute-start | bytes 1179656 | tf_op jit(solution)/shard_map/ppermute | solution.py:222
  17.3 4.3 %collective-permute-done.1.refs_1_ = f32[9,3,32,128]{3,2,1,0:T(8,128)S(1)} collective-permute-done((f32[9,3,32,128]{3,2,1,0:T(8,128)}, f32[9,3,32,128]{3,2,1,0:T(8,128)S(1)}, u32[]{:S(2)}, u32[]{:S(2)}) %collective-permute-start.1) | collective-permute-done | bytes 442400 | tf_op jit(solution)/shard_map/ppermute | solution.py:222
  21.9 17.8 %collective-permute-done.2.refs_2_ = f32[9,3,32,128]{3,2,1,0:T(8,128)S(1)} collective-permute-done((f32[9,3,32,128]{3,2,1,0:T(8,128)}, f32[9,3,32,128]{3,2,1,0:T(8,128)S(1)}, u32[]{:S(2)}, u32[]{:S(2)}) %collective-permute-start.2) | collective-permute-done | bytes 442400 | tf_op jit(solution)/shard_map/ppermute | solution.py:222
  39.8 2.0 %collective-permute-start.6 = (f32[8,3,32,128]{3,2,1,0:T(8,128)S(1)}, f32[8,3,32,128]{3,2,1,0:T(8,128)}, u32[]{:S(2)}, u32[]{:S(2)}) collective-permute-start(f32[8,3,32,128]{3,2,1,0:T(8,128)S(1)} %slice.17), channel_id=1, source_target_pairs={{0,28},{4,0},{8,4},{12,8},{16,12},{20,16},{24,20},{28,24},{1,29},{... | collective-permute-start | bytes 1179656 | tf_op jit(solution)/shard_map/ppermute | solution.py:222
  41.9 0.6 collective-permute-start.7
  42.6 29.4 %xz_part.1.run_ref = f32[4096,128]{1,0:T(8,128)} custom-call(s32[1]{0:T(128)} %bitcast.me_ref, f32[8,3,32,128]{3,2,1,0:T(8,128)} %chunks.2.test_ref, f32[9,3,32,128]{3,2,1,0:T(8,128)} %get-tuple-element.9.refs_0_, f32[9,3,32,128]{3,2,1,0:T(8,128)} %copy-done.1, f32[9,3,32,128]{3,2,1,0:T(8,128)} %copy-done.2, f32[9,3,32,128]{3,2,1,0:T(8,128)} %copy-done.3), custom_call_target="tpu_custom_call" | custom-call | flops 6442450944 | bytes 4194304 | tf_op jit(solution)/shard_map/xz_part/pallas_call | solution.py:201
  72.0 0.7 copy-done.4
  72.8 24.8 %y_part.1 = f32[4096,128]{1,0:T(8,128)} custom-call(s32[1]{0:T(128)} %bitcast.me_ref, f32[8,3,32,128]{3,2,1,0:T(8,128)} %chunks.2.test_ref, f32[8,3,32,128]{3,2,1,0:T(8,128)} %collective-permute-done.next_test_ref, f32[4096,128]{1,0:T(8,128)} %xz_part.1.run_ref, f32[9,3,32,128]{3,2,1,0:T(8,128)} %get-tuple-element.9.refs_0_, f32[9,3,32,128]{3,2,1,0:T(8,128)} %copy-done.1, ...), custom_call_target="tpu_custom_call" | custom-call | flops 6442450944 | bytes 4194304 | tf_op jit(solution)/shard_map/y_part/pallas_call | solution.py:201
  97.5 1.5 %constant_dynamic-slice_fusion.9 = (f32[4,128,128]{2,1,0:T(8,128)S(1)}, f32[4,128,128]{2,1,0:T(8,128)S(1)}, f32[4,128,128]{2,1,0:T(8,128)S(1)}, f32[4,128,128]{2...) fusion(f32[32,128,128]{2,1,0:T(8,128)} %bitcast.12, ...), kind=kLoop, calls=%fused_computation.11 | loop fusion | bytes 3670044 | tf_op jit(solution)/shard_map/dynamic_slice | solution.py:230
  99.1 0.6 collective-permute-start.14
  99.7 0.9 collective-permute-start.13
  100.6 1.5 %collective-permute-start.11 = (f32[4,128,128]{2,1,0:T(8,128)S(1)}, f32[4,128,128]{2,1,0:T(8,128)S(1)}, u32[]{:S(2)}, u32[]{:S(2)}) collective-permute-start(f32[4,128,128]{2,1,0:T(8,128)S(1)} %get-tuple-element.17), channel_id=1, source_target_pairs={{0,16},{4,20},{8,24},{12,28},{16,0},{20,4},{24,8},{28,12},{1,17},{... | collective-permute-start | bytes 786440 | tf_op jit(solution)/shard_map/ppermute | solution.py:222
  102.1 1.5 %collective-permute-start.10 = (f32[4,128,128]{2,1,0:T(8,128)S(1)}, f32[4,128,128]{2,1,0:T(8,128)S(1)}, u32[]{:S(2)}, u32[]{:S(2)}) collective-permute-start(f32[4,128,128]{2,1,0:T(8,128)S(1)} %get-tuple-element.18), channel_id=1, source_target_pairs={{0,12},{4,16},{8,20},{12,24},{16,28},{20,0},{24,4},{28,8},{1,13},{... | collective-permute-start | bytes 786440 | tf_op jit(solution)/shard_map/ppermute | solution.py:222
  103.6 2.9 %collective-permute-done.14 = f32[4,128,128]{2,1,0:T(8,128)S(1)} collective-permute-done((f32[4,128,128]{2,1,0:T(8,128)S(1)}, f32[4,128,128]{2,1,0:T(8,128)S(1)}, u32[]{:S(2)}, u32[]{:S(2)}) %collective-permute-start.14) | collective-permute-done | bytes 262176 | tf_op jit(solution)/shard_map/ppermute | solution.py:222
  106.5 0.8 collective-permute-start.9
  107.3 6.1 %collective-permute-done.13 = f32[4,128,128]{2,1,0:T(8,128)S(1)} collective-permute-done((f32[4,128,128]{2,1,0:T(8,128)S(1)}, f32[4,128,128]{2,1,0:T(8,128)S(1)}, u32[]{:S(2)}, u32[]{:S(2)}) %collective-permute-start.13) | collective-permute-done | bytes 262176 | tf_op jit(solution)/shard_map/ppermute | solution.py:222
  113.5 11.9 %collective-permute-done.11 = f32[4,128,128]{2,1,0:T(8,128)S(1)} collective-permute-done((f32[4,128,128]{2,1,0:T(8,128)S(1)}, f32[4,128,128]{2,1,0:T(8,128)S(1)}, u32[]{:S(2)}, u32[]{:S(2)}) %collective-permute-start.11) | collective-permute-done | bytes 262176 | tf_op jit(solution)/shard_map/ppermute | solution.py:222
  125.4 0.8 collective-permute-done.10
  126.1 1.1 add_add_fusion
  127.2 10.5 %collective-permute-start.17 = (f32[4,32,128]{2,1,0:T(8,128)S(1)}, f32[4,32,128]{2,1,0:T(8,128)S(1)}, u32[]{:S(2)}, u32[]{:S(2)}) collective-permute-start(f32[4,32,128]{2,1,0:T(8,128)S(1)} %get-tuple-element.21), channel_id=1, source_target_pairs={{0,3},{1,0},{2,1},{3,2},{4,7},{5,4},{6,5},{7,6},{8,11},{9,8},{10,9... | collective-permute-start | bytes 196616 | tf_op jit(solution)/shard_map/ppermute | solution.py:222
  137.7 0.2 collective-permute-start.16
  138.0 0.4 collective-permute-start.15
  138.4 1.3 collective-permute-done.17
  139.6 3.3 %collective-permute-done.16 = f32[4,32,128]{2,1,0:T(8,128)S(1)} collective-permute-done((f32[4,32,128]{2,1,0:T(8,128)S(1)}, f32[4,32,128]{2,1,0:T(8,128)S(1)}, u32[]{:S(2)}, u32[]{:S(2)}) %collective-permute-start.16) | collective-permute-done | bytes 65568 | tf_op jit(solution)/shard_map/ppermute | solution.py:222
  142.9 1.1 collective-permute-done.15
  144.0 0.6 add_add_fusion.1
  (26 shorter events, 0.6 us)
Async XLA Ops:
  5.2 10.6 %copy-start = (f32[9,3,32,128]{3,2,1,0:T(8,128)S(1)}, f32[9,3,32,128]{3,2,1,0:T(8,128)}, u32[]{:S(2)}) copy-start(f32[9,3,32,128]{3,2,1,0:T(8,128)} %get-tuple-element.9.refs_0_) | copy-start | bytes 1327108
  5.2 16.5 %collective-permute-start.1 = (f32[9,3,32,128]{3,2,1,0:T(8,128)}, f32[9,3,32,128]{3,2,1,0:T(8,128)S(1)}, u32[]{:S(2)}, u32[]{:S(2)}) collective-permute-start(f32[9,3,32,128]{3,2,1,0:T(8,128)} %get-tuple-element.10), channel_id=1, source_target_pairs={{0,1},{1,2},{2,3},{3,0},{4,5},{5,6},{6,7},{7,4},{8,9},{9,10},{10,1... | collective-permute-start | bytes 1327112 | tf_op jit(solution)/shard_map/ppermute | solution.py:222
  8.3 31.5 %collective-permute-start.2 = (f32[9,3,32,128]{3,2,1,0:T(8,128)}, f32[9,3,32,128]{3,2,1,0:T(8,128)S(1)}, u32[]{:S(2)}, u32[]{:S(2)}) collective-permute-start(f32[9,3,32,128]{3,2,1,0:T(8,128)} %get-tuple-element.11), channel_id=1, source_target_pairs={{0,2},{1,3},{2,0},{3,1},{4,6},{5,7},{6,4},{7,5},{8,10},{9,11},{10,... | collective-permute-start | bytes 1327112 | tf_op jit(solution)/shard_map/ppermute | solution.py:222
  10.9 31.0 %collective-permute-start.3 = (f32[9,3,32,128]{3,2,1,0:T(8,128)}, f32[9,3,32,128]{3,2,1,0:T(8,128)S(1)}, u32[]{:S(2)}, u32[]{:S(2)}) collective-permute-start(f32[9,3,32,128]{3,2,1,0:T(8,128)} %get-tuple-element.12), channel_id=1, source_target_pairs={{0,3},{1,0},{2,1},{3,2},{4,7},{5,4},{6,5},{7,6},{8,11},{9,8},{10,9... | collective-permute-start | bytes 1327112 | tf_op jit(solution)/shard_map/ppermute | solution.py:222
  14.6 57.3 %collective-permute-start = (f32[8,3,32,128]{3,2,1,0:T(8,128)}, f32[8,3,32,128]{3,2,1,0:T(8,128)}, u32[]{:S(2)}, u32[]{:S(2)}) collective-permute-start(f32[8,3,32,128]{3,2,1,0:T(8,128)} %chunks.2.test_ref), channel_id=1, source_target_pairs={{0,28},{4,0},{8,4},{12,8},{16,12},{20,16},{24,20},{28,24},{1,29},{... | collective-permute-start | bytes 1179656 | tf_op jit(solution)/shard_map/ppermute | solution.py:222
  15.8 56.2 %collective-permute-start.4 = (f32[8,3,32,128]{3,2,1,0:T(8,128)S(1)}, f32[8,3,32,128]{3,2,1,0:T(8,128)S(1)}, u32[]{:S(2)}, u32[]{:S(2)}) collective-permute-start(f32[8,3,32,128]{3,2,1,0:T(8,128)S(1)} %slice.12), channel_id=1, source_target_pairs={{0,28},{4,0},{8,4},{12,8},{16,12},{20,16},{24,20},{28,24},{1,29},{... | collective-permute-start | bytes 1179656 | tf_op jit(solution)/shard_map/ppermute | solution.py:222
  21.7 20.8 %copy-start.1 = (f32[9,3,32,128]{3,2,1,0:T(8,128)}, f32[9,3,32,128]{3,2,1,0:T(8,128)S(1)}, u32[]{:S(2)}) copy-start(f32[9,3,32,128]{3,2,1,0:T(8,128)S(1)} %collective-permute-done.1.refs_1_) | copy-start | bytes 1327108
  21.7 50.3 %collective-permute-start.5 = (f32[8,3,32,128]{3,2,1,0:T(8,128)S(1)}, f32[8,3,32,128]{3,2,1,0:T(8,128)}, u32[]{:S(2)}, u32[]{:S(2)}) collective-permute-start(f32[8,3,32,128]{3,2,1,0:T(8,128)S(1)} %slice.16), channel_id=1, source_target_pairs={{0,28},{4,0},{8,4},{12,8},{16,12},{20,16},{24,20},{28,24},{1,29},{... | collective-permute-start | bytes 1179656 | tf_op jit(solution)/shard_map/ppermute | solution.py:222
  39.8 2.7 %copy-start.2 = (f32[9,3,32,128]{3,2,1,0:T(8,128)}, f32[9,3,32,128]{3,2,1,0:T(8,128)S(1)}, u32[]{:S(2)}) copy-start(f32[9,3,32,128]{3,2,1,0:T(8,128)S(1)} %collective-permute-done.2.refs_2_) | copy-start | bytes 1327108
  39.8 32.2 %collective-permute-start.6 = (f32[8,3,32,128]{3,2,1,0:T(8,128)S(1)}, f32[8,3,32,128]{3,2,1,0:T(8,128)}, u32[]{:S(2)}, u32[]{:S(2)}) collective-permute-start(f32[8,3,32,128]{3,2,1,0:T(8,128)S(1)} %slice.17), channel_id=1, source_target_pairs={{0,28},{4,0},{8,4},{12,8},{16,12},{20,16},{24,20},{28,24},{1,29},{... | collective-permute-start | bytes 1179656 | tf_op jit(solution)/shard_map/ppermute | solution.py:222
  41.8 0.8 copy-start.3
  41.9 30.2 %collective-permute-start.7 = (f32[8,3,32,128]{3,2,1,0:T(8,128)S(1)}, f32[8,3,32,128]{3,2,1,0:T(8,128)}, u32[]{:S(2)}, u32[]{:S(2)}) collective-permute-start(f32[8,3,32,128]{3,2,1,0:T(8,128)S(1)} %slice.18), channel_id=1, source_target_pairs={{0,28},{4,0},{8,4},{12,8},{16,12},{20,16},{24,20},{28,24},{1,29},{... | collective-permute-start | bytes 1179656 | tf_op jit(solution)/shard_map/ppermute | solution.py:222
  72.0 0.8 copy-start.4
  99.1 7.4 %collective-permute-start.14 = (f32[4,128,128]{2,1,0:T(8,128)S(1)}, f32[4,128,128]{2,1,0:T(8,128)S(1)}, u32[]{:S(2)}, u32[]{:S(2)}) collective-permute-start(f32[4,128,128]{2,1,0:T(8,128)S(1)} %get-tuple-element.14), channel_id=1, source_target_pairs={{0,28},{4,0},{8,4},{12,8},{16,12},{20,16},{24,20},{28,24},{1,29},{... | collective-permute-start | bytes 786440 | tf_op jit(solution)/shard_map/ppermute | solution.py:222
  99.7 13.6 %collective-permute-start.13 = (f32[4,128,128]{2,1,0:T(8,128)S(1)}, f32[4,128,128]{2,1,0:T(8,128)S(1)}, u32[]{:S(2)}, u32[]{:S(2)}) collective-permute-start(f32[4,128,128]{2,1,0:T(8,128)S(1)} %get-tuple-element.15), channel_id=1, source_target_pairs={{0,24},{4,28},{8,0},{12,4},{16,8},{20,12},{24,16},{28,20},{1,25},{... | collective-permute-start | bytes 786440 | tf_op jit(solution)/shard_map/ppermute | solution.py:222
  100.6 12.9 %collective-permute-start.12 = (f32[4,128,128]{2,1,0:T(8,128)S(1)}, f32[4,128,128]{2,1,0:T(8,128)S(1)}, u32[]{:S(2)}, u32[]{:S(2)}) collective-permute-start(f32[4,128,128]{2,1,0:T(8,128)S(1)} %get-tuple-element.16), channel_id=1, source_target_pairs={{0,20},{4,24},{8,28},{12,0},{16,4},{20,8},{24,12},{28,16},{1,21},{... | collective-permute-start | bytes 786440 | tf_op jit(solution)/shard_map/ppermute | solution.py:222
  100.6 24.8 %collective-permute-start.11 = (f32[4,128,128]{2,1,0:T(8,128)S(1)}, f32[4,128,128]{2,1,0:T(8,128)S(1)}, u32[]{:S(2)}, u32[]{:S(2)}) collective-permute-start(f32[4,128,128]{2,1,0:T(8,128)S(1)} %get-tuple-element.17), channel_id=1, source_target_pairs={{0,16},{4,20},{8,24},{12,28},{16,0},{20,4},{24,8},{28,12},{1,17},{... | collective-permute-start | bytes 786440 | tf_op jit(solution)/shard_map/ppermute | solution.py:222
  102.1 24.0 %collective-permute-start.10 = (f32[4,128,128]{2,1,0:T(8,128)S(1)}, f32[4,128,128]{2,1,0:T(8,128)S(1)}, u32[]{:S(2)}, u32[]{:S(2)}) collective-permute-start(f32[4,128,128]{2,1,0:T(8,128)S(1)} %get-tuple-element.18), channel_id=1, source_target_pairs={{0,12},{4,16},{8,20},{12,24},{16,28},{20,0},{24,4},{28,8},{1,13},{... | collective-permute-start | bytes 786440 | tf_op jit(solution)/shard_map/ppermute | solution.py:222
  106.5 19.7 %collective-permute-start.9 = (f32[4,128,128]{2,1,0:T(8,128)S(1)}, f32[4,128,128]{2,1,0:T(8,128)S(1)}, u32[]{:S(2)}, u32[]{:S(2)}) collective-permute-start(f32[4,128,128]{2,1,0:T(8,128)S(1)} %get-tuple-element.19), channel_id=1, source_target_pairs={{0,8},{4,12},{8,16},{12,20},{16,24},{20,28},{24,0},{28,4},{1,9},{5... | collective-permute-start | bytes 786440 | tf_op jit(solution)/shard_map/ppermute | solution.py:222
  113.4 12.8 %collective-permute-start.8 = (f32[4,128,128]{2,1,0:T(8,128)S(1)}, f32[4,128,128]{2,1,0:T(8,128)S(1)}, u32[]{:S(2)}, u32[]{:S(2)}) collective-permute-start(f32[4,128,128]{2,1,0:T(8,128)S(1)} %get-tuple-element.13), channel_id=1, source_target_pairs={{0,4},{4,8},{8,12},{12,16},{16,20},{20,24},{24,28},{28,0},{1,5},{5... | collective-permute-start | bytes 786440 | tf_op jit(solution)/shard_map/ppermute | solution.py:222
  127.2 12.4 %collective-permute-start.17 = (f32[4,32,128]{2,1,0:T(8,128)S(1)}, f32[4,32,128]{2,1,0:T(8,128)S(1)}, u32[]{:S(2)}, u32[]{:S(2)}) collective-permute-start(f32[4,32,128]{2,1,0:T(8,128)S(1)} %get-tuple-element.21), channel_id=1, source_target_pairs={{0,3},{1,0},{2,1},{3,2},{4,7},{5,4},{6,5},{7,6},{8,11},{9,8},{10,9... | collective-permute-start | bytes 196616 | tf_op jit(solution)/shard_map/ppermute | solution.py:222
  137.7 5.2 %collective-permute-start.16 = (f32[4,32,128]{2,1,0:T(8,128)S(1)}, f32[4,32,128]{2,1,0:T(8,128)S(1)}, u32[]{:S(2)}, u32[]{:S(2)}) collective-permute-start(f32[4,32,128]{2,1,0:T(8,128)S(1)} %get-tuple-element.22), channel_id=1, source_target_pairs={{0,2},{1,3},{2,0},{3,1},{4,6},{5,7},{6,4},{7,5},{8,10},{9,11},{10,... | collective-permute-start | bytes 196616 | tf_op jit(solution)/shard_map/ppermute | solution.py:222
  138.0 6.1 %collective-permute-start.15 = (f32[4,32,128]{2,1,0:T(8,128)S(1)}, f32[4,32,128]{2,1,0:T(8,128)S(1)}, u32[]{:S(2)}, u32[]{:S(2)}) collective-permute-start(f32[4,32,128]{2,1,0:T(8,128)S(1)} %get-tuple-element.20), channel_id=1, source_target_pairs={{0,1},{1,2},{2,3},{3,0},{4,5},{5,6},{6,7},{7,4},{8,9},{9,10},{10,1... | collective-permute-start | bytes 196616 | tf_op jit(solution)/shard_map/ppermute | solution.py:222

commit v2 on v0

v2 whole, which is shorter than its diff:
```python
import math
from functools import partial

import jax
import jax.numpy as jnp
from jax import lax
from jax.experimental import pallas as pl
from jax.experimental.pallas import tpu as pltpu
from jax.sharding import PartitionSpec as P


LANES = 128
PITCH_PAD = 8
ROWS = 2
STAGES = 2


def flat_rows(field):
    count, comps, nz, rows, nx = field.shape
    tiles = nx // LANES
    split = field.reshape(count, comps, nz, rows, tiles, LANES)
    return split.transpose(0, 1, 2, 4, 3, 5).reshape(count, comps * nz * tiles * rows, LANES)


def lane_ids(count):
    return lax.broadcasted_iota(jnp.int32, (count, LANES), 1)


def spread_kernel(dims, stages, me_ref, src_ref, *refs):
    count, nz, rows, nx, chunk, parts = dims
    tiles = nx // LANES
    outs, scratch, hold, in_sems, out_sems = refs[:-4], refs[-4], refs[-3], refs[-2], refs[-1]
    depth = nz * tiles * rows
    pitch = depth + PITCH_PAD

    def arrival(a):
        target = scratch.at[a].reshape(count, pitch, LANES).at[:, pl.ds(0, depth), :]
        return pltpu.make_async_copy(src_ref.at[:, pl.ds(a * depth, depth), :], target, in_sems.at[a])

    for a in range(3):
        arrival(a).start()
    lane = lane_ids(count)
    edges = [edge_masks(lax.rem(lane + LANES - 4 * z, LANES), rows, chunk) for z in range(nz)]
    lows, highs = [low for low, _ in edges], [high for _, high in edges]

    def moved(value, amount):
        return value if amount % LANES == 0 else pltpu.roll(value, amount % LANES, 1)

    def one_comp(a, carry):
        arrival(a).wait()
        packed = [jnp.zeros((count, LANES), jnp.float32) for _ in range(parts)]
        for z in range(nz):
            lines = [
                [scratch[a, pl.ds((z * tiles + tile) * rows + y, count, stride=pitch), :] for y in range(rows)]
                for tile in range(tiles)
            ]
            for part in range(parts):
                offset = part * chunk % LANES
                value = jnp.zeros((count, LANES), jnp.float32)
                for y in range(rows):
                    mine = (lane >= y * chunk) & (lane < (y + 1) * chunk)
                    value = jnp.where(mine, moved(lines[part * chunk // LANES][y], y * chunk - offset), value)
                hold[part, z, a] = value
                after, before = (part + 1) % parts, (part - 1) % parts
                packed[after] = jnp.where(lows[z], moved(value, 4 * z - chunk), packed[after])
                packed[before] = jnp.where(highs[z], moved(value, 4 * z + chunk), packed[before])
        for part in range(parts):
            hold[part, nz, a] = packed[part]
        for copy in departures(a):
            copy.start()
        return carry

    def departures(a):
        copies = []
        for stage, (levels, halos) in enumerate(stages):
            for shift in range(parts):
                part = me_ref[0] ^ shift
                pieces = [(levels[0], len(levels), 0)] + ([(nz, 1, len(levels))] if halos else [])
                for piece, (start, size, at) in enumerate(pieces):
                    source = hold.at[part, pl.ds(start, size), a]
                    target = outs[stage * parts + shift].at[pl.ds(at, size), a]
                    copies.append(pltpu.make_async_copy(source, target, out_sems.at[a, stage * 2 + piece, shift]))
        return copies

    lax.fori_loop(0, 3, one_comp, 0)

    def finish(a, carry):
        for copy in departures(a):
            copy.wait()
        return carry

    lax.fori_loop(0, 3, finish, 0)


def edge_masks(lane, rows, chunk, width=2):
    low, high = None, None
    for y in range(rows):
        before, after = (y * chunk - width) % LANES, (y + 1) * chunk % LANES
        one = (lane >= before) & (lane < before + width)
        two = (lane >= after) & (lane < after + width)
        low, high = (one, two) if low is None else (low | one, high | two)
    return low, high


def spread(field, me, parts, stages):
    count, comps, nz, rows, nx = field.shape
    flat = flat_rows(field)
    dims = (count, nz, rows, nx, nx // parts, parts)
    shapes = [(len(levels) + (1 if halos else 0), comps, count, LANES) for levels, halos in stages for _ in range(parts)]
    outs = pl.pallas_call(
        partial(spread_kernel, dims, stages),
        out_shape=[jax.ShapeDtypeStruct(shape, jnp.float32) for shape in shapes],
        in_specs=[pl.BlockSpec(memory_space=pltpu.SMEM), pl.BlockSpec(memory_space=pl.ANY)],
        out_specs=[pl.BlockSpec(memory_space=pl.ANY) for _ in shapes],
        scratch_shapes=[
            pltpu.VMEM((comps, count * (flat.shape[1] // comps + PITCH_PAD), LANES), jnp.float32),
            pltpu.VMEM((parts, nz + 1, comps, count, LANES), jnp.float32),
            pltpu.SemaphoreType.DMA((comps,)),
            pltpu.SemaphoreType.DMA((comps, 2 * len(stages), parts)),
        ],
        compiler_params=pltpu.CompilerParams(vmem_limit_bytes=16 * 2**20),
        name="spread",
    )(me, flat)
    return [list(outs[at : at + parts]) for at in range(0, len(outs), parts)]


def own_kernel(dims, me_ref, src_ref, out_ref, scratch, sem):
    count, nz, rows, nx, chunk = dims
    tiles = nx // LANES
    depth = 3 * nz * tiles * rows
    pitch = depth + PITCH_PAD
    copy = pltpu.make_async_copy(src_ref, scratch.reshape(count, pitch, LANES).at[:, pl.ds(0, depth), :], sem)
    copy.start()
    copy.wait()
    lane = lane_ids(count)
    start = me_ref[0] * chunk
    tile, offset = start // LANES, lax.rem(start, LANES)
    for a in range(3):
        for z in range(nz):
            value = jnp.zeros((count, LANES), jnp.float32)
            for y in range(rows):
                line = scratch[pl.ds(((a * nz + z) * tiles + tile) * rows + y, count, stride=pitch), :]
                mine = (lane >= y * chunk) & (lane < (y + 1) * chunk)
                value = jnp.where(mine, pltpu.roll(line, lax.rem(y * chunk - offset + LANES, LANES), 1), value)
            out_ref[z, a] = value


def own_chunk(field, me, parts):
    count, comps, nz, rows, nx = field.shape
    flat = flat_rows(field)
    return pl.pallas_call(
        partial(own_kernel, (count, nz, rows, nx, nx // parts)),
        out_shape=jax.ShapeDtypeStruct((nz, comps, count, LANES), jnp.float32),
        in_specs=[pl.BlockSpec(memory_space=pltpu.SMEM), pl.BlockSpec(memory_space=pl.ANY)],
        scratch_shapes=[
            pltpu.VMEM((count * (flat.shape[1] + PITCH_PAD), LANES), jnp.float32),
            pltpu.SemaphoreType.DMA,
        ],
        compiler_params=pltpu.CompilerParams(vmem_limit_bytes=16 * 2**20),
        name="own_chunk",
    )(me, flat)


def split_pair(value):
    high = value.astype(jnp.bfloat16)
    return high, (value - high.astype(jnp.float32)).astype(jnp.bfloat16)


def x_grad(value, packed, z, chunk):
    lane = lane_ids(value.shape[0])
    edge = pltpu.roll(packed, LANES - 4 * z, 1) if z else packed
    diffs = []
    for width in (1, 2):
        low, high = edge_masks(lane, ROWS, chunk, width)
        ahead, behind = jnp.where(high, edge, value), jnp.where(low, edge, value)
        diffs.append(pltpu.roll(ahead, LANES - width, 1) - pltpu.roll(behind, width, 1))
    return 8.0 * diffs[0] - diffs[1]


def y_grads(own, ahead, chunk):
    first = lane_ids(own.shape[0]) < chunk

    def swapped(value):
        if 2 * chunk == LANES:
            return pltpu.roll(value, chunk, 1)
        return jnp.where(first, pltpu.roll(value, LANES - chunk, 1), pltpu.roll(value, chunk, 1))

    turned = 8.0 * swapped(own)
    mine = jnp.where(first, turned, 8.0 * swapped(ahead) - turned) - ahead
    theirs = own - jnp.where(first, turned, 0.0)
    return mine, theirs


def part_kernel(plan, steps, me_ref, *refs):
    parts, count, nz, chunk, group, span, xs, ys, zs, has_run, scale = plan
    total = parts * count
    near = {(z + step) % nz for z in zs for step in range(-2, 3)}
    stages = sorted({z // span for z in near | set(xs + ys)} | ({0} if xs else set()))
    next_stages = sorted({z // span for z in ys})
    refs = list(refs)
    test_ref = refs.pop(0)
    next_test_ref = refs.pop(0) if ys else None
    run_ref = refs.pop(0) if has_run else None
    fields = {stage: [refs.pop(0) for _ in range(parts)] for stage in stages}
    nexts = {stage: [refs.pop(0) for _ in range(parts)] for stage in next_stages}
    out_ref, grad_ref, join_ref, right_ref = refs
    slabs = [(test_ref, z) for z in xs]
    slabs += [item for z in ys for item in ((test_ref, z), (next_test_ref, z))]
    slabs += [(test_ref, z) for z in zs]

    def prepare():
        for shift in range(parts):
            at = pl.multiple_of((me_ref[0] ^ shift) * count, count)
            rows = pl.ds(at, count)

            def level(z, a):
                return fields[z // span][shift][z % span, a]

            def one_comp(a, carry):
                slab = 0
                for z in xs:
                    grad_ref[slab * 3 + a, rows, :] = x_grad(level(z, a), fields[0][shift][span, a], z, chunk)
                    slab += 1
                for z in ys:
                    mine, theirs = y_grads(level(z, a), nexts[z // span][shift][z % span, a], chunk)
                    grad_ref[slab * 3 + a, rows, :] = mine
                    grad_ref[slab * 3 + 3 + a, rows, :] = theirs
                    slab += 2
                for z in zs:
                    ahead = level((z + 1) % nz, a) - level((z - 1) % nz, a)
                    farther = level((z + 2) % nz, a) - level((z - 2) % nz, a)
                    grad_ref[slab * 3 + a, rows, :] = 8.0 * ahead - farther
                    slab += 1
                return carry

            lax.fori_loop(0, 3, one_comp, 0)
            slab = 0
            for z in xs:
                join_ref[slab, rows, :] = level(z, 0)
                slab += 1
            for z in ys:
                join_ref[slab, rows, :] = level(z, 1)
                join_ref[slab + 1, rows, :] = nexts[z // span][shift][z % span, 1]
                slab += 2
            for z in zs:
                join_ref[slab, rows, :] = level(z, 2)
                slab += 1

        def turn(slab, carry):
            high, low = split_pair(join_ref[slab].T)
            at = pl.ds(pl.multiple_of(slab * LANES, LANES), LANES)
            right_ref[at, pl.ds(0, total)] = high
            right_ref[at, pl.ds(total, total)] = low
            return carry

        lax.fori_loop(0, len(slabs), turn, 0)

    prepare()

    def one_step(step, carry):
        first = block_of(step, me_ref) * group
        dims = (((1,), (0,)), ((), ()))
        both, rest = None, None
        for start in range(0, len(slabs), 2):
            width = min(2, len(slabs) - start)
            highs, lows = [[] for _ in range(group)], [[] for _ in range(group)]
            for slab in range(start, start + width):
                source, z = slabs[slab]
                grads = [grad_ref[slab * 3 + a] for a in range(3)]
                for i in range(group):
                    tests = [source[z, a, pl.ds(first + i, 1), :] for a in range(3)]
                    high, low = split_pair(tests[0] * grads[0] + tests[1] * grads[1] + tests[2] * grads[2])
                    highs[i].append(high)
                    lows[i].append(low)
            high = jnp.concatenate([jnp.concatenate(row, 1) for row in highs], 0)
            low = jnp.concatenate([jnp.concatenate(row, 1) for row in lows], 0)
            right = right_ref[pl.ds(start * LANES, width * LANES), :]
            part = lax.dot_general(high, right, dims, preferred_element_type=jnp.float32)
            more = lax.dot_general(low, right[:, :total], dims, preferred_element_type=jnp.float32)
            both = part if both is None else both + part
            rest = more if rest is None else rest + more
        result = both[:, :total] + both[:, total:] + rest
        if has_run:
            result = result + run_ref[pl.ds(pl.multiple_of(first * total, group * total), group * total), :]
        out_ref[pl.ds(pl.multiple_of(step * group * total, group * total), group * total), :] = (
            result if scale is None else result * scale
        )
        return carry

    lax.fori_loop(0, steps, one_step, 0)


def block_of(step, me_ref):
    return me_ref[1] + me_ref[2] * (me_ref[3] ^ step)


def part_call(plan, order, steps, inputs, running=None):
    parts, count, _, _, group, _, xs, ys, zs, has_run, scale = plan
    total = parts * count
    slabs = len(xs) + 2 * len(ys) + len(zs)
    whole = pl.BlockSpec(memory_space=pltpu.VMEM)
    place = [value is running for value in inputs].index(True) + 1 if has_run and scale is None else None
    return pl.pallas_call(
        partial(part_kernel, plan, steps),
        in_specs=[pl.BlockSpec(memory_space=pltpu.SMEM)] + [whole] * len(inputs),
        out_specs=whole,
        scratch_shapes=[
            pltpu.VMEM((3 * slabs, total, LANES), jnp.float32),
            pltpu.VMEM((slabs, total, LANES), jnp.float32),
            pltpu.VMEM((slabs * LANES, 2 * total), jnp.bfloat16),
        ],
        out_shape=pltpu.VMEM((steps * group * total, total), jnp.float32)
        if place is not None or not has_run
        else jax.ShapeDtypeStruct((steps * group * total, total), jnp.float32),
        input_output_aliases={} if place is None else {place: 0},
        compiler_params=pltpu.CompilerParams(vmem_limit_bytes=16 * 2**20),
        cost_estimate=pl.CostEstimate(
            flops=6 * slabs * LANES * steps * group * total * total,
            transcendentals=0, bytes_accessed=8 * steps * group * total * total),
    )(order, *[pltpu.with_memory_space_constraint(value, pltpu.VMEM) for value in inputs])


def shifted(value, axis, shift):
    size = lax.axis_size(axis)
    return lax.ppermute(value, axis, [(i, (i + shift) % size) for i in range(size)])


def swapped_with(value, axis, other):
    return lax.ppermute(value, axis, [(i, i ^ other) for i in range(lax.axis_size(axis))])


def scattered(value, axis, dim):
    size, me = lax.axis_size(axis), lax.axis_index(axis)
    length = value.shape[dim] // size
    total = lax.dynamic_slice_in_dim(value, me * length, length, dim)
    for other in range(size - 1, 0, -1):
        block = lax.dynamic_slice_in_dim(value, (me ^ other) * length, length, dim)
        total = total + swapped_with(block, axis, other)
    return total


def per_device(test_modes, modes):
    count, _, nz, rows, nx = modes.shape
    tests = test_modes.shape[0]
    parts, slabs = lax.axis_size("mode"), lax.axis_size("space")
    chunk, group = nx // parts, tests // slabs
    assert rows == ROWS and rows * chunk <= LANES and parts & (parts - 1) == 0 and slabs & (slabs - 1) == 0 and nz % STAGES == 0
    span = nz // STAGES
    me = lax.axis_index("mode").astype(jnp.int32)
    place = lax.axis_index("space").astype(jnp.int32)
    plain = jnp.stack([me, 0, 1, 0]).astype(jnp.int32)
    scale = 1.0 / (12.0 * math.sqrt(nx * nz * rows * slabs))
    levels = [tuple(range(stage * span, (stage + 1) * span)) for stage in range(STAGES)]

    return exchange(test_modes, modes, plain, place, levels, (parts, count, nz, chunk, group, span), scale)


def exchange(test_modes, modes, plain, place, levels, dims, scale):
    parts, count, nz, _, group, span = dims
    total, slabs = parts * count, test_modes.shape[0] // group
    fields = spread(modes, plain, parts, tuple((levels[stage], stage == 0) for stage in range(STAGES)))
    for stage in range(STAGES):
        for other in range(parts - 1, 0, -1):
            fields[stage][other] = swapped_with(fields[stage][other], "mode", other)
    test = own_chunk(test_modes, plain, parts)
    next_test = shifted(test, "space", -1)
    nexts = []
    for stage in range(STAGES):
        nexts.append([shifted(field[:span], "space", -1) for field in fields[stage]])

    running = None
    for stage in range(STAGES - 1):
        for kind in ("x", "y"):
            held = fields[stage] if stage == 0 or kind == "y" else fields[0] + fields[stage]
            plan = dims + ((levels[stage], (), ()) if kind == "x" else ((), levels[stage], ()))
            plan += (running is not None, None)
            given = [test] + ([next_test] if kind == "y" else []) + ([running] if running is not None else [])
            given += held + nexts[stage] if kind == "y" else held
            running = part_call(plan, plain, slabs, given, running)
    plan = dims + (levels[-1], (), tuple(range(nz)), running is not None, None)
    given = [test] + ([running] if running is not None else []) + sum(fields, [])
    running = part_call(plan, plain, slabs, given, running)

    plan = dims + ((), levels[-1], (), True, scale)
    given = [test, next_test, running] + fields[-1] + nexts[-1]
    me = plain[0]
    chips = slabs // 2
    side, chip = place % 2, place // 2

    def last(core):
        order = jnp.stack([me, core, 2, chip]).astype(jnp.int32)
        value = part_call(plan, order, chips, given, running)
        return value.reshape(chips, group, total, total)

    other = last(1 - side)
    came = swapped_with(other, "space", 1)
    both = last(side)
    in_plane = both[0] + came[0]
    for turn in range(chips - 1, 0, -1):
        in_plane = in_plane + swapped_with(both[turn] + came[turn], "space", 2 * turn)
    return scattered(in_plane, "mode", 1)


def solution(mesh):
    in_specs = (P(None, None, None, "space", None), P("mode", None, None, "space", None))
    return jax.shard_map(
        per_device, mesh=mesh, in_specs=in_specs, out_specs=P("space", "mode", None), check_vma=False
    )
```

time: 230 us -> 117 us (0.51); the launches traced: 227 us -> 117 us
  waiting for transfers between devices: 90.5 us -> 31.5 us
  matrix products: 51.5 us -> 0 us
  Pallas kernels: 0 us -> 46.8 us
  local copies, waits for them, and re-layouts: 45.7 us -> 2.26 us
  starting transfers between devices: 3.41 us -> 34.9 us
  other arithmetic: 21.6 us -> 0.99 us
  between operations: 14 us -> 0.19 us
    all_gather x1 -> x0, waiting for transfers between devices: 58 us -> none  [per_device(): everything = lax.all_gather(mode_flat, 'mode', axis=0, tiled=True)]
    dot_general x2 -> x0, matrix products: 51.5 us -> none  [add_piece(): jnp.einsum('ikbc,jbc->ikj', weighted, piece_block, precision=lax.Precisio...]
    pallas_call x0 -> x7, Pallas kernels: none -> 46.8 us  [the longest x5 39.9 us: part_call(): pl.pallas_call(partial(part_kernel, plan, steps), in_specs=[pl.BlockSpec(...]
    reduce_scatter x1 -> x0, waiting for transfers between devices: 32.5 us -> none  [per_device(): lax.psum_scatter(partial_triad, 'space', scatter_dimension=0, tiled=True)]
    ppermute x2 -> x22, starting transfers between devices: 3.36 us -> 34.9 us  [the longest x13 27.8 us: swapped_with(): lax.ppermute(value, axis, [(i, i ^ other) for i in range(lax.axis_size(ax...]
    ppermute x2 -> x22, waiting for transfers between devices: 0.01 us -> 31.5 us  [the longest x13 31.4 us: swapped_with(): lax.ppermute(value, axis, [(i, i ^ other) for i in range(lax.axis_size(ax...]
    div x3 -> x0, other arithmetic: 15.7 us -> none  [the longest x2 8.86 us: central_diff(): return (8.0 * ahead - farther) / 12.0]
    div x5 -> x0, local copies, waits for them, and re-layouts: 11.4 us -> none  [the longest x4 9.66 us: central_diff(): return (8.0 * ahead - farther) / 12.0]
  transfers between devices with their start and end apart: 4 -> 22, of which waited for: 2 -> 6; matrix products, arithmetic and copies ran while one was open for 24% -> 1% of each run, Pallas kernels for 0% -> 30%
where the time goes in v2:
time: 117 us
  Pallas kernels  46.8 us (40%)
  starting transfers between devices  34.9 us (30%)
  waiting for transfers between devices  31.5 us (27%)
  local copies, waits for them, and re-layouts  2.26 us (2%)
    pallas_call x5, Pallas kernels, part_call(): pl.pallas_call(partial(part_kernel, plan, steps), in_specs=[pl.BlockSpec(...  39.9 us
    ppermute x13, waiting for transfers between devices, swapped_with(): lax.ppermute(value, axis, [(i, i ^ other) for i in range(lax.axis_size(ax...  31.4 us
    ppermute x13, starting transfers between devices, swapped_with(): lax.ppermute(value, axis, [(i, i ^ other) for i in range(lax.axis_size(ax...  27.8 us
    ppermute x9, starting transfers between devices, shifted(): lax.ppermute(value, axis, [(i, (i + shift) % size) for i in range(size)])  7.09 us
    pallas_call x1, Pallas kernels, spread(): pl.pallas_call(partial(spread_kernel, dims, stages), out_shape=[jax.Shape...  5.94 us
  transfers between devices with their start and end apart: 22, of which 6 were waited for; matrix products, arithmetic and copies ran while one was open for 1% of the time, Pallas kernels for 30%

profile of v2, /device:TPU:0, one launch (start us, length us, event | category | flops | bytes accessed | tf_op | source)
XLA Modules:
  0.0 116.6 jit_solution(4479449395889569642)
XLA Ops:
  0.1 1.4 %copy-done = f32[32,3,8,2,256]{4,3,2,1,0:T(2,128)S(1)} copy-done((f32[32,3,8,2,256]{4,3,2,1,0:T(2,128)S(1)}, f32[32,3,8,2,256]{4,3,2,1,0:T(2,128)}, u32[]{:S(2)}) %copy-start) | copy-done | bytes 1572888
  1.5 5.9 %spread.1 = (f32[5,3,32,128]{3,2,1,0:T(8,128)S(1)}, f32[5,3,32,128]{3,2,1,0:T(8,128)S(1)}, f32[5,3,32,128]{3,2,1,0:T(8,128)S(1)}, f32[5,3,32,128]{3,2,1,0:T(8,12...) custom-call(s32[4]{0:T(128)S(1)} %pad_add_fusion.2.me_ref, ...), custom_call_target="tpu_custom_call" | custom-call | tf_op jit(solution)/shard_map/spread/pallas_call | solution.py:110
  7.4 3.1 %collective-permute-start.1 = (f32[5,3,32,128]{3,2,1,0:T(8,128)S(1)}, f32[5,3,32,128]{3,2,1,0:T(8,128)S(1)}, u32[]{:S(2)}, u32[]{:S(2)}) collective-permute-start(f32[5,3,32,128]{3,2,1,0:T(8,128)S(1)} %get-tuple-element.14), channel_id=1, source_target_pairs={{0,1},{1,0},{2,3},{3,2},{4,5},{5,4},{6,7},{7,6},{8,9},{9,8},{10,11... | collective-permute-start | bytes 737288 | tf_op jit(solution)/shard_map/ppermute | solution.py:329
  10.6 2.6 %collective-permute-start.2 = (f32[5,3,32,128]{3,2,1,0:T(8,128)S(1)}, f32[5,3,32,128]{3,2,1,0:T(8,128)S(1)}, u32[]{:S(2)}, u32[]{:S(2)}) collective-permute-start(f32[5,3,32,128]{3,2,1,0:T(8,128)S(1)} %get-tuple-element.15), channel_id=1, source_target_pairs={{0,2},{1,3},{2,0},{3,1},{4,6},{5,7},{6,4},{7,5},{8,10},{9,11},{10,... | collective-permute-start | bytes 737288 | tf_op jit(solution)/shard_map/ppermute | solution.py:329
  13.1 0.7 slice.40
  13.9 1.3 %collective-permute-start.4 = (f32[4,3,32,128]{3,2,1,0:T(8,128)}, f32[4,3,32,128]{3,2,1,0:T(8,128)S(1)}, u32[]{:S(2)}, u32[]{:S(2)}) collective-permute-start(f32[4,3,32,128]{3,2,1,0:T(8,128)} %slice.40), channel_id=1, source_target_pairs={{0,28},{4,0},{8,4},{12,8},{16,12},{20,16},{24,20},{28,24},{1,29},{... | collective-permute-start | bytes 589832 | tf_op jit(solution)/shard_map/ppermute | solution.py:325
  15.2 3.5 %collective-permute-start.10 = (f32[4,3,32,128]{3,2,1,0:T(8,128)S(1)}, f32[4,3,32,128]{3,2,1,0:T(8,128)S(1)}, u32[]{:S(2)}, u32[]{:S(2)}) collective-permute-start(f32[4,3,32,128]{3,2,1,0:T(8,128)S(1)} %get-tuple-element.20), channel_id=1, source_target_pairs={{0,3},{1,2},{2,1},{3,0},{4,7},{5,6},{6,5},{7,4},{8,11},{9,10},{10,... | collective-permute-start | bytes 589832 | tf_op jit(solution)/shard_map/ppermute | solution.py:329
  18.7 2.3 %collective-permute-done.1.refs_2_.refs_4_.refs_3_ = f32[5,3,32,128]{3,2,1,0:T(8,128)S(1)} collective-permute-done((f32[5,3,32,128]{3,2,1,0:T(8,128)S(1)}, f32[5,3,32,128]{3,2,1,0:T(8,128)S(1)}, u32[]{:S(2)}, u32[]{:S(2)}) %collective-permute-start.1) | collective-permute-done | bytes 245792 | tf_op jit(solution)/shard_map/ppermute | solution.py:329
  21.0 0.9 own_chunk.1.refs_0_
  22.0 13.1 %collective-permute-done.2.refs_3_.refs_5_.refs_4_ = f32[5,3,32,128]{3,2,1,0:T(8,128)S(1)} collective-permute-done((f32[5,3,32,128]{3,2,1,0:T(8,128)S(1)}, f32[5,3,32,128]{3,2,1,0:T(8,128)S(1)}, u32[]{:S(2)}, u32[]{:S(2)}) %collective-permute-start.2) | collective-permute-done | bytes 245792 | tf_op jit(solution)/shard_map/ppermute | solution.py:329
  35.1 6.8 %collective-permute-start.9 = (f32[4,3,32,128]{3,2,1,0:T(8,128)S(1)}, f32[4,3,32,128]{3,2,1,0:T(8,128)S(1)}, u32[]{:S(2)}, u32[]{:S(2)}) collective-permute-start(f32[4,3,32,128]{3,2,1,0:T(8,128)S(1)} %get-tuple-element.19), channel_id=1, source_target_pairs={{0,2},{1,3},{2,0},{3,1},{4,6},{5,7},{6,4},{7,5},{8,10},{9,11},{10,... | collective-permute-start | bytes 589832 | tf_op jit(solution)/shard_map/ppermute | solution.py:329
  42.0 2.5 %collective-permute-start.6 = (f32[4,3,32,128]{3,2,1,0:T(8,128)S(1)}, f32[4,3,32,128]{3,2,1,0:T(8,128)S(1)}, u32[]{:S(2)}, u32[]{:S(2)}) collective-permute-start(f32[4,3,32,128]{3,2,1,0:T(8,128)S(1)} %slice.53), channel_id=1, source_target_pairs={{0,28},{4,0},{8,4},{12,8},{16,12},{20,16},{24,20},{28,24},{1,29},{... | collective-permute-start | bytes 589832 | tf_op jit(solution)/shard_map/ppermute | solution.py:325
  44.7 7.0 %shard_map.28.refs_2_ = f32[4096,128]{1,0:T(8,128)S(1)} custom-call(s32[4]{0:T(128)S(1)} %pad_add_fusion.2.me_ref, f32[8,3,32,128]{3,2,1,0:T(8,128)S(1)} %own_chunk.1.refs_0_, f32[5,3,32,128]{3,2,1,0:T(8,128)S(1)} %get-tuple-element.13.refs_1_.refs_3_.refs_2_, f32[5,3,32,128]{3,2,1,0:T(8,128)S(1)} %collective-permute-done.1.refs_2_.refs_4_.refs_3_, ...), custom_call_target="tpu_custom_call" | custom-call | flops 1610612736 | bytes 4194304 | tf_op jit(solution)/shard_map/pallas_call | solution.py:303
  51.7 0.7 collective-permute-start.11
  52.4 1.8 %collective-permute-start.12 = (f32[4,3,32,128]{3,2,1,0:T(8,128)S(1)}, f32[4,3,32,128]{3,2,1,0:T(8,128)S(1)}, u32[]{:S(2)}, u32[]{:S(2)}) collective-permute-start(f32[4,3,32,128]{3,2,1,0:T(8,128)S(1)} %collective-permute-done.8.refs_7_.refs_4_), channel_id=1, source_target_pairs={{0,28},{4,0},{8,4},{12,8},{16,12},{20,16},{24,20},{28,24},{1,29},{... | collective-permute-start | bytes 589832 | tf_op jit(solution)/shard_map/ppermute | solution.py:325
  54.2 0.6 collective-permute-start.14
  54.8 8.7 %shard_map.29.refs_1_ = f32[4096,128]{1,0:T(8,128)S(1)} custom-call(s32[4]{0:T(128)S(1)} %pad_add_fusion.2.me_ref, f32[8,3,32,128]{3,2,1,0:T(8,128)S(1)} %own_chunk.1.refs_0_, f32[8,3,32,128]{3,2,1,0:T(8,128)S(1)} %collective-permute-done.refs_1_, f32[4096,128]{1,0:T(8,128)S(1)} %shard_map.28.refs_2_, ...), custom_call_target="tpu_custom_call", output_to_operand_aliasing={{}: (3, {})} | custom-call | flops 3221225472 | bytes 4194304 | tf_op jit(solution)/shard_map/pallas_call | solution.py:303
  63.5 12.7 %shard_map.30.refs_2_ = f32[4096,128]{1,0:T(8,128)S(1)} custom-call(s32[4]{0:T(128)S(1)} %pad_add_fusion.2.me_ref, f32[8,3,32,128]{3,2,1,0:T(8,128)S(1)} %own_chunk.1.refs_0_, f32[4096,128]{1,0:T(8,128)S(1)} %shard_map.29.refs_1_, f32[5,3,32,128]{3,2,1,0:T(8,128)S(1)} %get-tuple-element.13.refs_1_.refs_3_.refs_2_, ...), custom_call_target="tpu_custom_call", output_to_operand_aliasing={{}: (2, {})} | custom-call | flops 4831838208 | bytes 4194304 | tf_op jit(solution)/shard_map/pallas_call | solution.py:303
  76.3 5.7 %shard_map.32 = f32[2048,128]{1,0:T(8,128)S(1)} custom-call(s32[4]{0:T(128)S(1)} %get-tuple-element.32.me_ref, f32[8,3,32,128]{3,2,1,0:T(8,128)S(1)} %own_chunk.1.refs_0_, f32[8,3,32,128]{3,2,1,0:T(8,128)S(1)} %collective-permute-done.refs_1_, f32[4096,128]{1,0:T(8,128)S(1)} %shard_map.30.refs_2_, f32[4,3,32,128]{3,2,1,0:T(8,128)S(1)} %get-tuple-element.17.refs_6_.refs_3_, ...), custom_call_target="tpu_custom_call" | custom-call | flops 1610612736 | bytes 2097152 | tf_op jit(solution)/shard_map/pallas_call | solution.py:303
  82.1 5.7 %shard_map.31 = f32[2048,128]{1,0:T(8,128)S(1)} custom-call(s32[4]{0:T(128)S(1)} %get-tuple-element.31.me_ref, f32[8,3,32,128]{3,2,1,0:T(8,128)S(1)} %own_chunk.1.refs_0_, f32[8,3,32,128]{3,2,1,0:T(8,128)S(1)} %collective-permute-done.refs_1_, f32[4096,128]{1,0:T(8,128)S(1)} %shard_map.30.refs_2_, f32[4,3,32,128]{3,2,1,0:T(8,128)S(1)} %get-tuple-element.17.refs_6_.refs_3_, ...), custom_call_target="tpu_custom_call" | custom-call | flops 1610612736 | bytes 2097152 | tf_op jit(solution)/shard_map/pallas_call | solution.py:303
  87.9 0.1 fusion.2
  88.1 1.5 %collective-permute-start.16 = (f32[4,128,128]{2,1,0:T(8,128)S(1)}, f32[4,128,128]{2,1,0:T(8,128)S(1)}, u32[]{:S(2)}, u32[]{:S(2)}) collective-permute-start(f32[4,128,128]{2,1,0:T(8,128)S(1)} %get-tuple-element.25), channel_id=1, source_target_pairs={{0,24},{4,28},{8,16},{12,20},{16,8},{20,12},{24,0},{28,4},{1,25},{... | collective-permute-start | bytes 786440 | tf_op jit(solution)/shard_map/ppermute | solution.py:329
  89.5 1.5 %collective-permute-start.17 = (f32[4,128,128]{2,1,0:T(8,128)S(1)}, f32[4,128,128]{2,1,0:T(8,128)S(1)}, u32[]{:S(2)}, u32[]{:S(2)}) collective-permute-start(f32[4,128,128]{2,1,0:T(8,128)S(1)} %get-tuple-element.27), channel_id=1, source_target_pairs={{0,16},{4,20},{8,24},{12,28},{16,0},{20,4},{24,8},{28,12},{1,17},{... | collective-permute-start | bytes 786440 | tf_op jit(solution)/shard_map/ppermute | solution.py:329
  91.1 0.5 collective-permute-start.18
  91.6 6.6 %collective-permute-done.16 = f32[4,128,128]{2,1,0:T(8,128)S(1)} collective-permute-done((f32[4,128,128]{2,1,0:T(8,128)S(1)}, f32[4,128,128]{2,1,0:T(8,128)S(1)}, u32[]{:S(2)}, u32[]{:S(2)}) %collective-permute-start.16) | collective-permute-done | bytes 262176 | tf_op jit(solution)/shard_map/ppermute | solution.py:329
  98.2 5.1 %collective-permute-done.17 = f32[4,128,128]{2,1,0:T(8,128)S(1)} collective-permute-done((f32[4,128,128]{2,1,0:T(8,128)S(1)}, f32[4,128,128]{2,1,0:T(8,128)S(1)}, u32[]{:S(2)}, u32[]{:S(2)}) %collective-permute-start.17) | collective-permute-done | bytes 262176 | tf_op jit(solution)/shard_map/ppermute | solution.py:329
  103.5 2.5 %collective-permute-start.19 = (f32[4,32,128]{2,1,0:T(8,128)S(1)}, f32[4,32,128]{2,1,0:T(8,128)S(1)}, u32[]{:S(2)}, u32[]{:S(2)}) collective-permute-start(f32[4,32,128]{2,1,0:T(8,128)S(1)} %get-tuple-element.28), channel_id=1, source_target_pairs={{0,3},{1,2},{2,1},{3,0},{4,7},{5,6},{6,5},{7,4},{8,11},{9,10},{10,... | collective-permute-start | bytes 196616 | tf_op jit(solution)/shard_map/ppermute | solution.py:329
  106.0 5.5 %collective-permute-start.20 = (f32[4,32,128]{2,1,0:T(8,128)S(1)}, f32[4,32,128]{2,1,0:T(8,128)S(1)}, u32[]{:S(2)}, u32[]{:S(2)}) collective-permute-start(f32[4,32,128]{2,1,0:T(8,128)S(1)} %get-tuple-element.30), channel_id=1, source_target_pairs={{0,2},{1,3},{2,0},{3,1},{4,6},{5,7},{6,4},{7,5},{8,10},{9,11},{10,... | collective-permute-start | bytes 196616 | tf_op jit(solution)/shard_map/ppermute | solution.py:329
  111.5 0.1 collective-permute-start.21
  111.6 3.6 %collective-permute-done.20 = f32[4,32,128]{2,1,0:T(8,128)S(1)} collective-permute-done((f32[4,32,128]{2,1,0:T(8,128)S(1)}, f32[4,32,128]{2,1,0:T(8,128)S(1)}, u32[]{:S(2)}, u32[]{:S(2)}) %collective-permute-start.20) | collective-permute-done | bytes 65568 | tf_op jit(solution)/shard_map/ppermute | solution.py:329
  115.2 0.7 collective-permute-done.21
  115.9 0.6 add_add_fusion
  (34 shorter events, 0.7 us)
Async XLA Ops:
  0.1 1.4 %copy-start = (f32[32,3,8,2,256]{4,3,2,1,0:T(2,128)S(1)}, f32[32,3,8,2,256]{4,3,2,1,0:T(2,128)}, u32[]{:S(2)}) copy-start(f32[32,3,8,2,256]{4,3,2,1,0:T(2,128)} %param.3) | copy-start | bytes 4718596
  1.5 19.6 %copy-start.1 = (f32[32,3,8,2,256]{4,3,2,1,0:T(2,128)S(1)}, f32[32,3,8,2,256]{4,3,2,1,0:T(2,128)}, u32[]{:S(2)}) copy-start(f32[32,3,8,2,256]{4,3,2,1,0:T(2,128)} %param.2) | copy-start | bytes 4718596
  7.4 13.6 %collective-permute-start.1 = (f32[5,3,32,128]{3,2,1,0:T(8,128)S(1)}, f32[5,3,32,128]{3,2,1,0:T(8,128)S(1)}, u32[]{:S(2)}, u32[]{:S(2)}) collective-permute-start(f32[5,3,32,128]{3,2,1,0:T(8,128)S(1)} %get-tuple-element.14), channel_id=1, source_target_pairs={{0,1},{1,0},{2,3},{3,2},{4,5},{5,4},{6,7},{7,6},{8,9},{9,8},{10,11... | collective-permute-start | bytes 737288 | tf_op jit(solution)/shard_map/ppermute | solution.py:329
  10.6 24.5 %collective-permute-start.2 = (f32[5,3,32,128]{3,2,1,0:T(8,128)S(1)}, f32[5,3,32,128]{3,2,1,0:T(8,128)S(1)}, u32[]{:S(2)}, u32[]{:S(2)}) collective-permute-start(f32[5,3,32,128]{3,2,1,0:T(8,128)S(1)} %get-tuple-element.15), channel_id=1, source_target_pairs={{0,2},{1,3},{2,0},{3,1},{4,6},{5,7},{6,4},{7,5},{8,10},{9,11},{10,... | collective-permute-start | bytes 737288 | tf_op jit(solution)/shard_map/ppermute | solution.py:329
  13.1 22.0 %collective-permute-start.3 = (f32[5,3,32,128]{3,2,1,0:T(8,128)S(1)}, f32[5,3,32,128]{3,2,1,0:T(8,128)S(1)}, u32[]{:S(2)}, u32[]{:S(2)}) collective-permute-start(f32[5,3,32,128]{3,2,1,0:T(8,128)S(1)} %get-tuple-element.16), channel_id=1, source_target_pairs={{0,3},{1,2},{2,1},{3,0},{4,7},{5,6},{6,5},{7,4},{8,11},{9,10},{10,... | collective-permute-start | bytes 737288 | tf_op jit(solution)/shard_map/ppermute | solution.py:329
  13.9 28.1 %collective-permute-start.4 = (f32[4,3,32,128]{3,2,1,0:T(8,128)}, f32[4,3,32,128]{3,2,1,0:T(8,128)S(1)}, u32[]{:S(2)}, u32[]{:S(2)}) collective-permute-start(f32[4,3,32,128]{3,2,1,0:T(8,128)} %slice.40), channel_id=1, source_target_pairs={{0,28},{4,0},{8,4},{12,8},{16,12},{20,16},{24,20},{28,24},{1,29},{... | collective-permute-start | bytes 589832 | tf_op jit(solution)/shard_map/ppermute | solution.py:325
  15.2 26.8 %collective-permute-start.10 = (f32[4,3,32,128]{3,2,1,0:T(8,128)S(1)}, f32[4,3,32,128]{3,2,1,0:T(8,128)S(1)}, u32[]{:S(2)}, u32[]{:S(2)}) collective-permute-start(f32[4,3,32,128]{3,2,1,0:T(8,128)S(1)} %get-tuple-element.20), channel_id=1, source_target_pairs={{0,3},{1,2},{2,1},{3,0},{4,7},{5,6},{6,5},{7,4},{8,11},{9,10},{10,... | collective-permute-start | bytes 589832 | tf_op jit(solution)/shard_map/ppermute | solution.py:329
  21.0 23.5 %collective-permute-start.8 = (f32[4,3,32,128]{3,2,1,0:T(8,128)S(1)}, f32[4,3,32,128]{3,2,1,0:T(8,128)S(1)}, u32[]{:S(2)}, u32[]{:S(2)}) collective-permute-start(f32[4,3,32,128]{3,2,1,0:T(8,128)S(1)} %get-tuple-element.18), channel_id=1, source_target_pairs={{0,1},{1,0},{2,3},{3,2},{4,5},{5,4},{6,7},{7,6},{8,9},{9,8},{10,11... | collective-permute-start | bytes 589832 | tf_op jit(solution)/shard_map/ppermute | solution.py:329
  35.1 17.3 %collective-permute-start = (f32[8,3,32,128]{3,2,1,0:T(8,128)S(1)}, f32[8,3,32,128]{3,2,1,0:T(8,128)S(1)}, u32[]{:S(2)}, u32[]{:S(2)}) collective-permute-start(f32[8,3,32,128]{3,2,1,0:T(8,128)S(1)} %own_chunk.1.refs_0_), channel_id=1, source_target_pairs={{0,28},{4,0},{8,4},{12,8},{16,12},{20,16},{24,20},{28,24},{1,29},{... | collective-permute-start | bytes 1179656 | tf_op jit(solution)/shard_map/ppermute | solution.py:325
  35.1 16.6 %collective-permute-start.9 = (f32[4,3,32,128]{3,2,1,0:T(8,128)S(1)}, f32[4,3,32,128]{3,2,1,0:T(8,128)S(1)}, u32[]{:S(2)}, u32[]{:S(2)}) collective-permute-start(f32[4,3,32,128]{3,2,1,0:T(8,128)S(1)} %get-tuple-element.19), channel_id=1, source_target_pairs={{0,2},{1,3},{2,0},{3,1},{4,6},{5,7},{6,4},{7,5},{8,10},{9,11},{10,... | collective-permute-start | bytes 589832 | tf_op jit(solution)/shard_map/ppermute | solution.py:329
  41.9 12.2 %collective-permute-start.5 = (f32[4,3,32,128]{3,2,1,0:T(8,128)S(1)}, f32[4,3,32,128]{3,2,1,0:T(8,128)S(1)}, u32[]{:S(2)}, u32[]{:S(2)}) collective-permute-start(f32[4,3,32,128]{3,2,1,0:T(8,128)S(1)} %slice.52), channel_id=1, source_target_pairs={{0,28},{4,0},{8,4},{12,8},{16,12},{20,16},{24,20},{28,24},{1,29},{... | collective-permute-start | bytes 589832 | tf_op jit(solution)/shard_map/ppermute | solution.py:325
  42.0 12.2 %collective-permute-start.6 = (f32[4,3,32,128]{3,2,1,0:T(8,128)S(1)}, f32[4,3,32,128]{3,2,1,0:T(8,128)S(1)}, u32[]{:S(2)}, u32[]{:S(2)}) collective-permute-start(f32[4,3,32,128]{3,2,1,0:T(8,128)S(1)} %slice.53), channel_id=1, source_target_pairs={{0,28},{4,0},{8,4},{12,8},{16,12},{20,16},{24,20},{28,24},{1,29},{... | collective-permute-start | bytes 589832 | tf_op jit(solution)/shard_map/ppermute | solution.py:325
  44.6 10.3 %collective-permute-start.7 = (f32[4,3,32,128]{3,2,1,0:T(8,128)S(1)}, f32[4,3,32,128]{3,2,1,0:T(8,128)S(1)}, u32[]{:S(2)}, u32[]{:S(2)}) collective-permute-start(f32[4,3,32,128]{3,2,1,0:T(8,128)S(1)} %slice.54), channel_id=1, source_target_pairs={{0,28},{4,0},{8,4},{12,8},{16,12},{20,16},{24,20},{28,24},{1,29},{... | collective-permute-start | bytes 589832 | tf_op jit(solution)/shard_map/ppermute | solution.py:325
  51.7 24.6 %collective-permute-start.11 = (f32[4,3,32,128]{3,2,1,0:T(8,128)S(1)}, f32[4,3,32,128]{3,2,1,0:T(8,128)S(1)}, u32[]{:S(2)}, u32[]{:S(2)}) collective-permute-start(f32[4,3,32,128]{3,2,1,0:T(8,128)S(1)} %get-tuple-element.17.refs_6_.refs_3_), channel_id=1, source_target_pairs={{0,28},{4,0},{8,4},{12,8},{16,12},{20,16},{24,20},{28,24},{1,29},{... | collective-permute-start | bytes 589832 | tf_op jit(solution)/shard_map/ppermute | solution.py:325
  52.4 23.9 %collective-permute-start.12 = (f32[4,3,32,128]{3,2,1,0:T(8,128)S(1)}, f32[4,3,32,128]{3,2,1,0:T(8,128)S(1)}, u32[]{:S(2)}, u32[]{:S(2)}) collective-permute-start(f32[4,3,32,128]{3,2,1,0:T(8,128)S(1)} %collective-permute-done.8.refs_7_.refs_4_), channel_id=1, source_target_pairs={{0,28},{4,0},{8,4},{12,8},{16,12},{20,16},{24,20},{28,24},{1,29},{... | collective-permute-start | bytes 589832 | tf_op jit(solution)/shard_map/ppermute | solution.py:325
  54.2 22.1 %collective-permute-start.13 = (f32[4,3,32,128]{3,2,1,0:T(8,128)S(1)}, f32[4,3,32,128]{3,2,1,0:T(8,128)S(1)}, u32[]{:S(2)}, u32[]{:S(2)}) collective-permute-start(f32[4,3,32,128]{3,2,1,0:T(8,128)S(1)} %collective-permute-done.9.refs_8_.refs_5_), channel_id=1, source_target_pairs={{0,28},{4,0},{8,4},{12,8},{16,12},{20,16},{24,20},{28,24},{1,29},{... | collective-permute-start | bytes 589832 | tf_op jit(solution)/shard_map/ppermute | solution.py:325
  54.2 22.1 %collective-permute-start.14 = (f32[4,3,32,128]{3,2,1,0:T(8,128)S(1)}, f32[4,3,32,128]{3,2,1,0:T(8,128)S(1)}, u32[]{:S(2)}, u32[]{:S(2)}) collective-permute-start(f32[4,3,32,128]{3,2,1,0:T(8,128)S(1)} %collective-permute-done.10.refs_9_.refs_6_), channel_id=1, source_target_pairs={{0,28},{4,0},{8,4},{12,8},{16,12},{20,16},{24,20},{28,24},{1,29},{... | collective-permute-start | bytes 589832 | tf_op jit(solution)/shard_map/ppermute | solution.py:325
  82.1 5.9 %collective-permute-start.15 = (f32[4,4,128,128]{3,2,1,0:T(8,128)S(1)}, f32[4,4,128,128]{3,2,1,0:T(8,128)S(1)}, u32[]{:S(2)}, u32[]{:S(2)}) collective-permute-start(f32[4,4,128,128]{3,2,1,0:T(8,128)S(1)} %bitcast.43), channel_id=1, source_target_pairs={{0,4},{4,0},{8,12},{12,8},{16,20},{20,16},{24,28},{28,24},{1,5},{5... | collective-permute-start | bytes 3145736 | tf_op jit(solution)/shard_map/ppermute | solution.py:329
  88.1 10.2 %collective-permute-start.16 = (f32[4,128,128]{2,1,0:T(8,128)S(1)}, f32[4,128,128]{2,1,0:T(8,128)S(1)}, u32[]{:S(2)}, u32[]{:S(2)}) collective-permute-start(f32[4,128,128]{2,1,0:T(8,128)S(1)} %get-tuple-element.25), channel_id=1, source_target_pairs={{0,24},{4,28},{8,16},{12,20},{16,8},{20,12},{24,0},{28,4},{1,25},{... | collective-permute-start | bytes 786440 | tf_op jit(solution)/shard_map/ppermute | solution.py:329
  89.5 13.8 %collective-permute-start.17 = (f32[4,128,128]{2,1,0:T(8,128)S(1)}, f32[4,128,128]{2,1,0:T(8,128)S(1)}, u32[]{:S(2)}, u32[]{:S(2)}) collective-permute-start(f32[4,128,128]{2,1,0:T(8,128)S(1)} %get-tuple-element.27), channel_id=1, source_target_pairs={{0,16},{4,20},{8,24},{12,28},{16,0},{20,4},{24,8},{28,12},{1,17},{... | collective-permute-start | bytes 786440 | tf_op jit(solution)/shard_map/ppermute | solution.py:329
  91.1 12.3 %collective-permute-start.18 = (f32[4,128,128]{2,1,0:T(8,128)S(1)}, f32[4,128,128]{2,1,0:T(8,128)S(1)}, u32[]{:S(2)}, u32[]{:S(2)}) collective-permute-start(f32[4,128,128]{2,1,0:T(8,128)S(1)} %get-tuple-element.26), channel_id=1, source_target_pairs={{0,8},{4,12},{8,0},{12,4},{16,24},{20,28},{24,16},{28,20},{1,9},{5... | collective-permute-start | bytes 786440 | tf_op jit(solution)/shard_map/ppermute | solution.py:329
  103.5 8.2 %collective-permute-start.19 = (f32[4,32,128]{2,1,0:T(8,128)S(1)}, f32[4,32,128]{2,1,0:T(8,128)S(1)}, u32[]{:S(2)}, u32[]{:S(2)}) collective-permute-start(f32[4,32,128]{2,1,0:T(8,128)S(1)} %get-tuple-element.28), channel_id=1, source_target_pairs={{0,3},{1,2},{2,1},{3,0},{4,7},{5,6},{6,5},{7,4},{8,11},{9,10},{10,... | collective-permute-start | bytes 196616 | tf_op jit(solution)/shard_map/ppermute | solution.py:329
  106.0 9.2 %collective-permute-start.20 = (f32[4,32,128]{2,1,0:T(8,128)S(1)}, f32[4,32,128]{2,1,0:T(8,128)S(1)}, u32[]{:S(2)}, u32[]{:S(2)}) collective-permute-start(f32[4,32,128]{2,1,0:T(8,128)S(1)} %get-tuple-element.30), channel_id=1, source_target_pairs={{0,2},{1,3},{2,0},{3,1},{4,6},{5,7},{6,4},{7,5},{8,10},{9,11},{10,... | collective-permute-start | bytes 196616 | tf_op jit(solution)/shard_map/ppermute | solution.py:329
  111.5 4.4 %collective-permute-start.21 = (f32[4,32,128]{2,1,0:T(8,128)S(1)}, f32[4,32,128]{2,1,0:T(8,128)S(1)}, u32[]{:S(2)}, u32[]{:S(2)}) collective-permute-start(f32[4,32,128]{2,1,0:T(8,128)S(1)} %get-tuple-element.29), channel_id=1, source_target_pairs={{0,1},{1,0},{2,3},{3,2},{4,5},{5,4},{6,7},{7,6},{8,9},{9,8},{10,11... | collective-permute-start | bytes 196616 | tf_op jit(solution)/shard_map/ppermute | solution.py:329

commit v3 on v2

--- a/solution.py
+++ b/solution.py
@@ -29,7 +29,7 @@
 def spread_kernel(dims, stages, me_ref, src_ref, *refs):
     count, nz, rows, nx, chunk, parts = dims
     tiles = nx // LANES
-    outs, scratch, hold, in_sems, out_sems = refs[:-4], refs[-4], refs[-3], refs[-2], refs[-1]
+    outs, scratch, hold, in_sems = refs[:-3], refs[-3], refs[-2], refs[-1]
     depth = nz * tiles * rows
     pitch = depth + PITCH_PAD
 
@@ -60,44 +60,32 @@
                 for y in range(rows):
                     mine = (lane >= y * chunk) & (lane < (y + 1) * chunk)
                     value = jnp.where(mine, moved(lines[part * chunk // LANES][y], y * chunk - offset), value)
-                hold[part, z, a] = value
+                hold[part, z] = value
                 after, before = (part + 1) % parts, (part - 1) % parts
-                packed[after] = jnp.where(lows[z], moved(value, 4 * z - chunk), packed[after])
-                packed[before] = jnp.where(highs[z], moved(value, 4 * z + chunk), packed[before])
+                back = moved(value, 4 * z - chunk)
+                on = back if 2 * chunk % LANES == 0 else moved(value, 4 * z + chunk)
+                packed[after] = jnp.where(lows[z], back, packed[after])
+                packed[before] = jnp.where(highs[z], on, packed[before])
         for part in range(parts):
-            hold[part, nz, a] = packed[part]
-        for copy in departures(a):
-            copy.start()
-        return carry
-
-    def departures(a):
-        copies = []
-        for stage, (levels, halos) in enumerate(stages):
+            hold[part, nz] = packed[part]
+        index = 0
+        for levels, halos in stages:
             for shift in range(parts):
                 part = me_ref[0] ^ shift
-                pieces = [(levels[0], len(levels), 0)] + ([(nz, 1, len(levels))] if halos else [])
-                for piece, (start, size, at) in enumerate(pieces):
-                    source = hold.at[part, pl.ds(start, size), a]
-                    target = outs[stage * parts + shift].at[pl.ds(at, size), a]
-                    copies.append(pltpu.make_async_copy(source, target, out_sems.at[a, stage * 2 + piece, shift]))
-        return copies
+                for place, z in enumerate(levels + ((nz,) if halos else ())):
+                    outs[index][place, a] = hold[part, z]
+                index += 1
+        return carry
 
     lax.fori_loop(0, 3, one_comp, 0)
 
-    def finish(a, carry):
-        for copy in departures(a):
-            copy.wait()
-        return carry
-
-    lax.fori_loop(0, 3, finish, 0)
-
-
-def edge_masks(lane, rows, chunk, width=2):
+
+def edge_masks(lane, rows, chunk):
     low, high = None, None
     for y in range(rows):
-        before, after = (y * chunk - width) % LANES, (y + 1) * chunk % LANES
-        one = (lane >= before) & (lane < before + width)
-        two = (lane >= after) & (lane < after + width)
+        before, after = (y * chunk - 2) % LANES, (y + 1) * chunk % LANES
+        one = (lane >= before) & (lane < before + 2)
+        two = (lane >= after) & (lane < after + 2)
         low, high = (one, two) if low is None else (low | one, high | two)
     return low, high
 
@@ -109,18 +97,17 @@
     shapes = [(len(levels) + (1 if halos else 0), comps, count, LANES) for levels, halos in stages for _ in range(parts)]
     outs = pl.pallas_call(
         partial(spread_kernel, dims, stages),
-        out_shape=[jax.ShapeDtypeStruct(shape, jnp.float32) for shape in shapes],
-        in_specs=[pl.BlockSpec(memory_space=pltpu.SMEM), pl.BlockSpec(memory_space=pl.ANY)],
-        out_specs=[pl.BlockSpec(memory_space=pl.ANY) for _ in shapes],
+        out_shape=[pltpu.VMEM(shape, jnp.float32) for shape in shapes],
+        in_specs=[pl.BlockSpec(memory_space=pltpu.SMEM), pl.BlockSpec(memory_space=pltpu.HBM)],
+        out_specs=[pl.BlockSpec(memory_space=pltpu.VMEM) for _ in shapes],
         scratch_shapes=[
             pltpu.VMEM((comps, count * (flat.shape[1] // comps + PITCH_PAD), LANES), jnp.float32),
-            pltpu.VMEM((parts, nz + 1, comps, count, LANES), jnp.float32),
+            pltpu.VMEM((parts, nz + 1, count, LANES), jnp.float32),
             pltpu.SemaphoreType.DMA((comps,)),
-            pltpu.SemaphoreType.DMA((comps, 2 * len(stages), parts)),
         ],
         compiler_params=pltpu.CompilerParams(vmem_limit_bytes=16 * 2**20),
         name="spread",
-    )(me, flat)
+    )(me, pltpu.with_memory_space_constraint(flat, pltpu.HBM))
     return [list(outs[at : at + parts]) for at in range(0, len(outs), parts)]
 
 
@@ -151,14 +138,14 @@
     return pl.pallas_call(
         partial(own_kernel, (count, nz, rows, nx, nx // parts)),
         out_shape=jax.ShapeDtypeStruct((nz, comps, count, LANES), jnp.float32),
-        in_specs=[pl.BlockSpec(memory_space=pltpu.SMEM), pl.BlockSpec(memory_space=pl.ANY)],
+        in_specs=[pl.BlockSpec(memory_space=pltpu.SMEM), pl.BlockSpec(memory_space=pltpu.HBM)],
         scratch_shapes=[
             pltpu.VMEM((count * (flat.shape[1] + PITCH_PAD), LANES), jnp.float32),
             pltpu.SemaphoreType.DMA,
         ],
         compiler_params=pltpu.CompilerParams(vmem_limit_bytes=16 * 2**20),
         name="own_chunk",
-    )(me, flat)
+    )(me, pltpu.with_memory_space_constraint(flat, pltpu.HBM))
 
 
 def split_pair(value):
@@ -166,15 +153,28 @@
     return high, (value - high.astype(jnp.float32)).astype(jnp.bfloat16)
 
 
-def x_grad(value, packed, z, chunk):
-    lane = lane_ids(value.shape[0])
-    edge = pltpu.roll(packed, LANES - 4 * z, 1) if z else packed
-    diffs = []
-    for width in (1, 2):
-        low, high = edge_masks(lane, ROWS, chunk, width)
-        ahead, behind = jnp.where(high, edge, value), jnp.where(low, edge, value)
-        diffs.append(pltpu.roll(ahead, LANES - width, 1) - pltpu.roll(behind, width, 1))
-    return 8.0 * diffs[0] - diffs[1]
+def x_band(z, chunk):
+    row = lax.broadcasted_iota(jnp.int32, (LANES, LANES), 0)
+    column = lax.broadcasted_iota(jnp.int32, (LANES, LANES), 1)
+    bands = []
+    for source, inside in ((row, True), (lax.rem(row + LANES - 4 * z, LANES), False)):
+        gap = lax.rem(source - column + LANES + LANES // 2, LANES) - LANES // 2
+        near = jnp.where(gap == 1, 8.0, jnp.where(gap == -1, -8.0, 0.0))
+        band = jnp.where(gap == 2, -1.0, jnp.where(gap == -2, 1.0, near))
+        same = source // chunk == column // chunk
+        bands.append(jnp.where(same if inside else ~same, band, 0.0))
+    return jnp.concatenate(bands, 0).astype(jnp.bfloat16)
+
+
+def x_grads(values, packed, z, chunk):
+    band = x_band(z, chunk)
+    total = None
+    for piece in zip(split_pair(values), split_pair(packed)):
+        part = lax.dot_general(
+            jnp.concatenate(piece, 1), band, (((1,), (0,)), ((), ())), preferred_element_type=jnp.float32
+        )
+        total = part if total is None else total + part
+    return total
 
 
 def y_grads(own, ahead, chunk):
@@ -192,7 +192,7 @@
 
 
 def part_kernel(plan, steps, me_ref, *refs):
-    parts, count, nz, chunk, group, span, xs, ys, zs, has_run, scale = plan
+    parts, count, nz, chunk, group, span, xs, ys, zs, has_run, scale, tables = plan
     total = parts * count
     near = {(z + step) % nz for z in zs for step in range(-2, 3)}
     stages = sorted({z // span for z in near | set(xs + ys)} | ({0} if xs else set()))
@@ -201,26 +201,43 @@
     test_ref = refs.pop(0)
     next_test_ref = refs.pop(0) if ys else None
     run_ref = refs.pop(0) if has_run else None
-    fields = {stage: [refs.pop(0) for _ in range(parts)] for stage in stages}
-    nexts = {stage: [refs.pop(0) for _ in range(parts)] for stage in next_stages}
-    out_ref, grad_ref, join_ref, right_ref = refs
+    if tables != "given":
+        fields = {stage: [refs.pop(0) for _ in range(parts)] for stage in stages}
+        nexts = {stage: [refs.pop(0) for _ in range(parts)] for stage in next_stages}
+    if tables == "keep":
+        out_ref, grad_ref, right_ref, join_ref = refs
+    elif tables == "given":
+        grad_ref, right_ref, out_ref = refs
+    else:
+        out_ref, grad_ref, join_ref, right_ref = refs
     slabs = [(test_ref, z) for z in xs]
     slabs += [item for z in ys for item in ((test_ref, z), (next_test_ref, z))]
     slabs += [(test_ref, z) for z in zs]
 
+    def place(shift):
+        return pl.ds(pl.multiple_of((me_ref[0] ^ shift) * count, count), count)
+
+    def prepare_x():
+        packed = jnp.concatenate([fields[0][shift][span].reshape(3 * count, LANES) for shift in range(parts)], 0)
+        for slab, z in enumerate(xs):
+            values = [fields[z // span][shift][z % span].reshape(3 * count, LANES) for shift in range(parts)]
+            grads = x_grads(jnp.concatenate(values, 0), packed, z, chunk)
+            for shift in range(parts):
+                for a in range(3):
+                    at = (shift * 3 + a) * count
+                    grad_ref[slab * 3 + a, place(shift), :] = grads[at : at + count]
+
     def prepare():
+        if xs:
+            prepare_x()
         for shift in range(parts):
-            at = pl.multiple_of((me_ref[0] ^ shift) * count, count)
-            rows = pl.ds(at, count)
+            rows = place(shift)
 
             def level(z, a):
                 return fields[z // span][shift][z % span, a]
 
             def one_comp(a, carry):
-                slab = 0
-                for z in xs:
-                    grad_ref[slab * 3 + a, rows, :] = x_grad(level(z, a), fields[0][shift][span, a], z, chunk)
-                    slab += 1
+                slab = len(xs)
                 for z in ys:
                     mine, theirs = y_grads(level(z, a), nexts[z // span][shift][z % span, a], chunk)
                     grad_ref[slab * 3 + a, rows, :] = mine
@@ -233,7 +250,8 @@
                     slab += 1
                 return carry
 
-            lax.fori_loop(0, 3, one_comp, 0)
+            if ys or zs:
+                lax.fori_loop(0, 3, one_comp, 0)
             slab = 0
             for z in xs:
                 join_ref[slab, rows, :] = level(z, 0)
@@ -255,7 +273,8 @@
 
         lax.fori_loop(0, len(slabs), turn, 0)
 
-    prepare()
+    if tables != "given":
+        prepare()
 
     def one_step(step, carry):
         first = block_of(step, me_ref) * group
@@ -287,7 +306,7 @@
         )
         return carry
 
-    lax.fori_loop(0, steps, one_step, 0)
+    lax.fori_loop(0, steps, one_step, 0, unroll=2)
 
 
 def block_of(step, me_ref):
@@ -295,23 +314,22 @@
 
 
 def part_call(plan, order, steps, inputs, running=None):
-    parts, count, _, _, group, _, xs, ys, zs, has_run, scale = plan
+    parts, count, _, _, group, _, xs, ys, zs, has_run, scale, tables = plan
     total = parts * count
     slabs = len(xs) + 2 * len(ys) + len(zs)
     whole = pl.BlockSpec(memory_space=pltpu.VMEM)
     place = [value is running for value in inputs].index(True) + 1 if has_run and scale is None else None
+    out = pltpu.VMEM((steps * group * total, total), jnp.float32)
+    grads = pltpu.VMEM((3 * slabs, total, LANES), jnp.float32)
+    joined = pltpu.VMEM((slabs, total, LANES), jnp.float32)
+    rights = pltpu.VMEM((slabs * LANES, 2 * total), jnp.bfloat16)
+    outs, scratch = {"": ([out], [grads, joined, rights]), "keep": ([out, grads, rights], [joined]), "given": ([out], [])}[tables]
     return pl.pallas_call(
         partial(part_kernel, plan, steps),
         in_specs=[pl.BlockSpec(memory_space=pltpu.SMEM)] + [whole] * len(inputs),
-        out_specs=whole,
-        scratch_shapes=[
-            pltpu.VMEM((3 * slabs, total, LANES), jnp.float32),
-            pltpu.VMEM((slabs, total, LANES), jnp.float32),
-            pltpu.VMEM((slabs * LANES, 2 * total), jnp.bfloat16),
-        ],
-        out_shape=pltpu.VMEM((steps * group * total, total), jnp.float32)
-        if place is not None or not has_run
-        else jax.ShapeDtypeStruct((steps * group * total, total), jnp.float32),
+        out_specs=[whole] * len(outs),
+        out_shape=outs,
+        scratch_shapes=scratch,
         input_output_aliases={} if place is None else {place: 0},
         compiler_params=pltpu.CompilerParams(vmem_limit_bytes=16 * 2**20),
         cost_estimate=pl.CostEstimate(
@@ -373,31 +391,38 @@
         for kind in ("x", "y"):
             held = fields[stage] if stage == 0 or kind == "y" else fields[0] + fields[stage]
             plan = dims + ((levels[stage], (), ()) if kind == "x" else ((), levels[stage], ()))
-            plan += (running is not None, None)
+            plan += (running is not None, None, "")
             given = [test] + ([next_test] if kind == "y" else []) + ([running] if running is not None else [])
             given += held + nexts[stage] if kind == "y" else held
-            running = part_call(plan, plain, slabs, given, running)
-    plan = dims + (levels[-1], (), tuple(range(nz)), running is not None, None)
+            running = part_call(plan, plain, slabs, given, running)[0]
+    plan = dims + (levels[-1], (), tuple(range(nz)), running is not None, None, "")
     given = [test] + ([running] if running is not None else []) + sum(fields, [])
-    running = part_call(plan, plain, slabs, given, running)
-
-    plan = dims + ((), levels[-1], (), True, scale)
-    given = [test, next_test, running] + fields[-1] + nexts[-1]
+    running = part_call(plan, plain, slabs, given, running)[0]
+
     me = plain[0]
-    chips = slabs // 2
-    side, chip = place % 2, place // 2
-
-    def last(core):
-        order = jnp.stack([me, core, 2, chip]).astype(jnp.int32)
-        value = part_call(plan, order, chips, given, running)
-        return value.reshape(chips, group, total, total)
-
-    other = last(1 - side)
-    came = swapped_with(other, "space", 1)
-    both = last(side)
-    in_plane = both[0] + came[0]
-    for turn in range(chips - 1, 0, -1):
-        in_plane = in_plane + swapped_with(both[turn] + came[turn], "space", 2 * turn)
+    side, chip, half = place % 2, place // 2, slabs // 4
+
+    def last(core, start, steps, tables, given):
+        plan = dims + ((), levels[-1], (), True, scale, tables)
+        order = jnp.stack([me, core, 2, start]).astype(jnp.int32)
+        value, *held = part_call(plan, order, steps, [test, next_test, running] + given, running)
+        return value.reshape(steps, group, total, total), held
+
+    far_start = chip ^ half
+    value, held = last(1 - side, far_start, half, "keep", fields[-1] + nexts[-1])
+    far_came = swapped_with(value, "space", 1)
+    value, _ = last(1 - side, chip, half, "given", held)
+    came = swapped_with(value, "space", 1)
+    far, _ = last(side, far_start, half, "given", held)
+    sent = [None] * half
+    for step in range(half - 1, -1, -1):
+        sent[step] = swapped_with(far[step] + far_came[step], "space", 2 * (half + step))
+    near, _ = last(side, chip, half, "given", held)
+    in_plane = near[0] + came[0]
+    for step in range(half - 1, 0, -1):
+        in_plane = in_plane + swapped_with(near[step] + came[step], "space", 2 * step)
+    for value in sent:
+        in_plane = in_plane + value
     return scattered(in_plane, "mode", 1)
 
 

time: 117 us -> 109 us (0.932)
  Pallas kernels: 46.8 us -> 41.9 us
  starting transfers between devices: 34.9 us -> 32.9 us
  local copies, waits for them, and re-layouts: 2.26 us -> 0.84 us
    pallas_call x5 -> x7, Pallas kernels: 39.9 us -> 34 us  [part_call(): pl.pallas_call(partial(part_kernel, plan, steps), in_specs=[pl.BlockSpec(...]
    ppermute x13 -> x14, starting transfers between devices: 27.8 us -> 25.7 us  [swapped_with(): lax.ppermute(value, axis, [(i, i ^ other) for i in range(lax.axis_size(ax...]
    unnamed x4 -> x0, local copies, waits for them, and re-layouts: 1.41 us -> none
    pallas_call x1, Pallas kernels: 0.94 us -> 2.23 us  [own_chunk(): pl.pallas_call(partial(own_kernel, (count, nz, rows, nx, nx // parts)), o...]
    ppermute x13 -> x14, waiting for transfers between devices: 31.4 us -> 32.4 us  [swapped_with(): lax.ppermute(value, axis, [(i, i ^ other) for i in range(lax.axis_size(ax...]
  transfers between devices with their start and end apart: 22 -> 23, of which waited for: 6 -> 8; matrix products, arithmetic and copies ran while one was open for 1% -> 1% of each run, Pallas kernels for 30% -> 28%
where the time goes in v3:
time: 109 us
  Pallas kernels  41.9 us (38%)
  starting transfers between devices  32.9 us (30%)
  waiting for transfers between devices  32.4 us (30%)
    pallas_call x7, Pallas kernels, part_call(): pl.pallas_call(partial(part_kernel, plan, steps), in_specs=[pl.BlockSpec(...  34 us
    ppermute x14, waiting for transfers between devices, swapped_with(): lax.ppermute(value, axis, [(i, i ^ other) for i in range(lax.axis_size(ax...  32.4 us
    ppermute x14, starting transfers between devices, swapped_with(): lax.ppermute(value, axis, [(i, i ^ other) for i in range(lax.axis_size(ax...  25.7 us
    ppermute x9, starting transfers between devices, shifted(): lax.ppermute(value, axis, [(i, (i + shift) % size) for i in range(size)])  7.2 us
    pallas_call x1, Pallas kernels, spread(): pl.pallas_call(partial(spread_kernel, dims, stages), out_shape=[pltpu.VME...  5.67 us
    pallas_call x1, Pallas kernels, own_chunk(): pl.pallas_call(partial(own_kernel, (count, nz, rows, nx, nx // parts)), o...  2.23 us
  transfers between devices with their start and end apart: 23, of which 8 were waited for; matrix products, arithmetic and copies ran while one was open for 1% of the time, Pallas kernels for 28%

profile of v3, /device:TPU:0, one launch (start us, length us, event | category | flops | bytes accessed | tf_op | source)
XLA Modules:
  0.0 109.3 jit_solution(9615300472442971494)
XLA Ops:
  0.1 5.7 %spread.1 = (f32[5,3,32,128]{3,2,1,0:T(8,128)S(1)}, f32[5,3,32,128]{3,2,1,0:T(8,128)S(1)}, f32[5,3,32,128]{3,2,1,0:T(8,128)S(1)}, f32[5,3,32,128]{3,2,1,0:T(8,12...) custom-call(s32[4]{0:T(128)S(1)} %pad_add_fusion.2.me_ref, ...), custom_call_target="tpu_custom_call" | custom-call | tf_op jit(solution)/shard_map/spread/pallas_call | solution.py:98
  5.8 3.1 %collective-permute-start.1 = (f32[5,3,32,128]{3,2,1,0:T(8,128)S(1)}, f32[5,3,32,128]{3,2,1,0:T(8,128)S(1)}, u32[]{:S(2)}, u32[]{:S(2)}) collective-permute-start(f32[5,3,32,128]{3,2,1,0:T(8,128)S(1)} %get-tuple-element.17), channel_id=1, source_target_pairs={{0,1},{1,0},{2,3},{3,2},{4,5},{5,4},{6,7},{7,6},{8,9},{9,8},{10,11... | collective-permute-start | bytes 737288 | tf_op jit(solution)/shard_map/ppermute | solution.py:347
  8.9 2.6 %collective-permute-start.2 = (f32[5,3,32,128]{3,2,1,0:T(8,128)S(1)}, f32[5,3,32,128]{3,2,1,0:T(8,128)S(1)}, u32[]{:S(2)}, u32[]{:S(2)}) collective-permute-start(f32[5,3,32,128]{3,2,1,0:T(8,128)S(1)} %get-tuple-element.18), channel_id=1, source_target_pairs={{0,2},{1,3},{2,0},{3,1},{4,6},{5,7},{6,4},{7,5},{8,10},{9,11},{10,... | collective-permute-start | bytes 737288 | tf_op jit(solution)/shard_map/ppermute | solution.py:347
  11.5 0.7 slice.40
  12.2 1.3 %collective-permute-start.4 = (f32[4,3,32,128]{3,2,1,0:T(8,128)}, f32[4,3,32,128]{3,2,1,0:T(8,128)S(1)}, u32[]{:S(2)}, u32[]{:S(2)}) collective-permute-start(f32[4,3,32,128]{3,2,1,0:T(8,128)} %slice.40), channel_id=1, source_target_pairs={{0,28},{4,0},{8,4},{12,8},{16,12},{20,16},{24,20},{28,24},{1,29},{... | collective-permute-start | bytes 589832 | tf_op jit(solution)/shard_map/ppermute | solution.py:343
  13.5 3.5 %collective-permute-start.10 = (f32[4,3,32,128]{3,2,1,0:T(8,128)S(1)}, f32[4,3,32,128]{3,2,1,0:T(8,128)S(1)}, u32[]{:S(2)}, u32[]{:S(2)}) collective-permute-start(f32[4,3,32,128]{3,2,1,0:T(8,128)S(1)} %get-tuple-element.23), channel_id=1, source_target_pairs={{0,3},{1,2},{2,1},{3,0},{4,7},{5,6},{6,5},{7,4},{8,11},{9,10},{10,... | collective-permute-start | bytes 589832 | tf_op jit(solution)/shard_map/ppermute | solution.py:347
  17.0 2.3 %collective-permute-done.1.refs_2_.refs_4_.refs_3_ = f32[5,3,32,128]{3,2,1,0:T(8,128)S(1)} collective-permute-done((f32[5,3,32,128]{3,2,1,0:T(8,128)S(1)}, f32[5,3,32,128]{3,2,1,0:T(8,128)S(1)}, u32[]{:S(2)}, u32[]{:S(2)}) %collective-permute-start.1) | collective-permute-done | bytes 245792 | tf_op jit(solution)/shard_map/ppermute | solution.py:347
  19.4 2.2 %own_chunk.1.refs_0_ = f32[8,3,32,128]{3,2,1,0:T(8,128)S(1)} custom-call(s32[4]{0:T(128)S(1)} %pad_add_fusion.2.me_ref, f32[32,96,128]{2,1,0:T(8,128)} %bitcast.46), custom_call_target="tpu_custom_call" | custom-call | tf_op jit(solution)/shard_map/own_chunk/pallas_call | solution.py:138
  21.6 11.8 %collective-permute-done.2.refs_3_.refs_5_.refs_4_ = f32[5,3,32,128]{3,2,1,0:T(8,128)S(1)} collective-permute-done((f32[5,3,32,128]{3,2,1,0:T(8,128)S(1)}, f32[5,3,32,128]{3,2,1,0:T(8,128)S(1)}, u32[]{:S(2)}, u32[]{:S(2)}) %collective-permute-start.2) | collective-permute-done | bytes 245792 | tf_op jit(solution)/shard_map/ppermute | solution.py:347
  33.5 6.7 %collective-permute-start.9 = (f32[4,3,32,128]{3,2,1,0:T(8,128)S(1)}, f32[4,3,32,128]{3,2,1,0:T(8,128)S(1)}, u32[]{:S(2)}, u32[]{:S(2)}) collective-permute-start(f32[4,3,32,128]{3,2,1,0:T(8,128)S(1)} %get-tuple-element.22), channel_id=1, source_target_pairs={{0,2},{1,3},{2,0},{3,1},{4,6},{5,7},{6,4},{7,5},{8,10},{9,11},{10,... | collective-permute-start | bytes 589832 | tf_op jit(solution)/shard_map/ppermute | solution.py:347
  40.3 2.5 %collective-permute-start.6 = (f32[4,3,32,128]{3,2,1,0:T(8,128)S(1)}, f32[4,3,32,128]{3,2,1,0:T(8,128)S(1)}, u32[]{:S(2)}, u32[]{:S(2)}) collective-permute-start(f32[4,3,32,128]{3,2,1,0:T(8,128)S(1)} %slice.53), channel_id=1, source_target_pairs={{0,28},{4,0},{8,4},{12,8},{16,12},{20,16},{24,20},{28,24},{1,29},{... | collective-permute-start | bytes 589832 | tf_op jit(solution)/shard_map/ppermute | solution.py:343
  43.0 4.9 %shard_map.28.refs_2_ = f32[4096,128]{1,0:T(8,128)S(1)} custom-call(s32[4]{0:T(128)S(1)} %pad_add_fusion.2.me_ref, f32[8,3,32,128]{3,2,1,0:T(8,128)S(1)} %own_chunk.1.refs_0_, f32[5,3,32,128]{3,2,1,0:T(8,128)S(1)} %get-tuple-element.16.refs_1_.refs_3_.refs_2_, f32[5,3,32,128]{3,2,1,0:T(8,128)S(1)} %collective-permute-done.1.refs_2_.refs_4_.refs_3_, ...), custom_call_target="tpu_custom_call" | custom-call | flops 1610612736 | bytes 4194304 | tf_op jit(solution)/shard_map/pallas_call | solution.py:327
  47.9 2.0 %collective-permute-done.9.refs_8_.refs_5_ = f32[4,3,32,128]{3,2,1,0:T(8,128)S(1)} collective-permute-done((f32[4,3,32,128]{3,2,1,0:T(8,128)S(1)}, f32[4,3,32,128]{3,2,1,0:T(8,128)S(1)}, u32[]{:S(2)}, u32[]{:S(2)}) %collective-permute-start.9) | collective-permute-done | bytes 196640 | tf_op jit(solution)/shard_map/ppermute | solution.py:347
  49.9 0.8 collective-permute-start.11
  50.7 1.8 %collective-permute-start.12 = (f32[4,3,32,128]{3,2,1,0:T(8,128)S(1)}, f32[4,3,32,128]{3,2,1,0:T(8,128)S(1)}, u32[]{:S(2)}, u32[]{:S(2)}) collective-permute-start(f32[4,3,32,128]{3,2,1,0:T(8,128)S(1)} %collective-permute-done.8.refs_7_.refs_4_), channel_id=1, source_target_pairs={{0,28},{4,0},{8,4},{12,8},{16,12},{20,16},{24,20},{28,24},{1,29},{... | collective-permute-start | bytes 589832 | tf_op jit(solution)/shard_map/ppermute | solution.py:343
  52.6 0.6 collective-permute-start.14
  53.2 8.3 %shard_map.29.refs_1_ = f32[4096,128]{1,0:T(8,128)S(1)} custom-call(s32[4]{0:T(128)S(1)} %pad_add_fusion.2.me_ref, f32[8,3,32,128]{3,2,1,0:T(8,128)S(1)} %own_chunk.1.refs_0_, f32[8,3,32,128]{3,2,1,0:T(8,128)S(1)} %collective-permute-done.refs_1_, f32[4096,128]{1,0:T(8,128)S(1)} %shard_map.28.refs_2_, ...), custom_call_target="tpu_custom_call", output_to_operand_aliasing={{}: (3, {})} | custom-call | flops 3221225472 | bytes 4194304 | tf_op jit(solution)/shard_map/pallas_call | solution.py:327
  61.4 11.0 %shard_map.30.refs_2_ = f32[4096,128]{1,0:T(8,128)S(1)} custom-call(s32[4]{0:T(128)S(1)} %pad_add_fusion.2.me_ref, f32[8,3,32,128]{3,2,1,0:T(8,128)S(1)} %own_chunk.1.refs_0_, f32[4096,128]{1,0:T(8,128)S(1)} %shard_map.29.refs_1_, f32[5,3,32,128]{3,2,1,0:T(8,128)S(1)} %get-tuple-element.16.refs_1_.refs_3_.refs_2_, ...), custom_call_target="tpu_custom_call", output_to_operand_aliasing={{}: (2, {})} | custom-call | flops 4831838208 | bytes 4194304 | tf_op jit(solution)/shard_map/pallas_call | solution.py:327
  72.4 4.1 %shard_map.31 = (f32[1024,128]{1,0:T(8,128)S(1)}, f32[24,128,128]{2,1,0:T(8,128)S(1)}, bf16[1024,256]{1,0:T(8,128)(2,1)S(1)}) custom-call(s32[4]{0:T(128)S(1)} %get-tuple-element.39.me_ref, f32[8,3,32,128]{3,2,1,0:T(8,128)S(1)} %own_chunk.1.refs_0_, f32[8,3,32,128]{3,2,1,0:T(8,128)S(1)} %collective-permute-done.refs_1_, f32[4096,128]{1,0:T(8,128)S(1)} %shard_map.30.refs_2_, ...), custom_call_target="tpu_custom_call" | custom-call | flops 805306368 | bytes 1048576 | tf_op jit(solution)/shard_map/pallas_call | solution.py:327
  76.5 2.0 %shard_map.33 = f32[1024,128]{1,0:T(8,128)S(1)} custom-call(s32[4]{0:T(128)S(1)} %get-tuple-element.36.me_ref, f32[8,3,32,128]{3,2,1,0:T(8,128)S(1)} %own_chunk.1.refs_0_, f32[8,3,32,128]{3,2,1,0:T(8,128)S(1)} %collective-permute-done.refs_1_, f32[4096,128]{1,0:T(8,128)S(1)} %shard_map.30.refs_2_, f32[24,128,128]{2,1,0:T(8,128)S(1)} %get-tuple-element.24.refs_3_, ...), custom_call_target="tpu_custom_call" | custom-call | flops 805306368 | bytes 1048576 | tf_op jit(solution)/shard_map/pallas_call | solution.py:327
  79.1 2.0 %shard_map.32 = f32[1024,128]{1,0:T(8,128)S(1)} custom-call(s32[4]{0:T(128)S(1)} %get-tuple-element.37.me_ref, f32[8,3,32,128]{3,2,1,0:T(8,128)S(1)} %own_chunk.1.refs_0_, f32[8,3,32,128]{3,2,1,0:T(8,128)S(1)} %collective-permute-done.refs_1_, f32[4096,128]{1,0:T(8,128)S(1)} %shard_map.30.refs_2_, f32[24,128,128]{2,1,0:T(8,128)S(1)} %get-tuple-element.24.refs_3_, ...), custom_call_target="tpu_custom_call" | custom-call | flops 805306368 | bytes 1048576 | tf_op jit(solution)/shard_map/pallas_call | solution.py:327
  81.1 2.0 %shard_map.34 = f32[1024,128]{1,0:T(8,128)S(1)} custom-call(s32[4]{0:T(128)S(1)} %get-tuple-element.38.me_ref, f32[8,3,32,128]{3,2,1,0:T(8,128)S(1)} %own_chunk.1.refs_0_, f32[8,3,32,128]{3,2,1,0:T(8,128)S(1)} %collective-permute-done.refs_1_, f32[4096,128]{1,0:T(8,128)S(1)} %shard_map.30.refs_2_, f32[24,128,128]{2,1,0:T(8,128)S(1)} %get-tuple-element.24.refs_3_, ...), custom_call_target="tpu_custom_call" | custom-call | flops 805306368 | bytes 1048576 | tf_op jit(solution)/shard_map/pallas_call | solution.py:327
  83.1 1.5 %collective-permute-start.16 = (f32[4,128,128]{2,1,0:T(8,128)S(1)}, f32[4,128,128]{2,1,0:T(8,128)S(1)}, u32[]{:S(2)}, u32[]{:S(2)}) collective-permute-start(f32[4,128,128]{2,1,0:T(8,128)S(1)} %fusion.2), channel_id=1, source_target_pairs={{0,8},{4,12},{8,0},{12,4},{16,24},{20,28},{24,16},{28,20},{1,9},{5... | collective-permute-start | bytes 786440 | tf_op jit(solution)/shard_map/ppermute | solution.py:347
  85.3 1.5 %collective-permute-start.19 = (f32[4,128,128]{2,1,0:T(8,128)S(1)}, f32[4,128,128]{2,1,0:T(8,128)S(1)}, u32[]{:S(2)}, u32[]{:S(2)}) collective-permute-start(f32[4,128,128]{2,1,0:T(8,128)S(1)} %get-tuple-element.30), channel_id=1, source_target_pairs={{0,24},{4,28},{8,16},{12,20},{16,8},{20,12},{24,0},{28,4},{1,25},{... | collective-permute-start | bytes 786440 | tf_op jit(solution)/shard_map/ppermute | solution.py:347
  86.8 5.6 %collective-permute-done.16 = f32[4,128,128]{2,1,0:T(8,128)S(1)} collective-permute-done((f32[4,128,128]{2,1,0:T(8,128)S(1)}, f32[4,128,128]{2,1,0:T(8,128)S(1)}, u32[]{:S(2)}, u32[]{:S(2)}) %collective-permute-start.16) | collective-permute-done | bytes 262176 | tf_op jit(solution)/shard_map/ppermute | solution.py:347
  92.4 6.1 %collective-permute-done.18 = f32[4,128,128]{2,1,0:T(8,128)S(1)} collective-permute-done((f32[4,128,128]{2,1,0:T(8,128)S(1)}, f32[4,128,128]{2,1,0:T(8,128)S(1)}, u32[]{:S(2)}, u32[]{:S(2)}) %collective-permute-start.18) | collective-permute-done | bytes 262176 | tf_op jit(solution)/shard_map/ppermute | solution.py:347
  98.5 2.6 %collective-permute-start.20 = (f32[4,32,128]{2,1,0:T(8,128)S(1)}, f32[4,32,128]{2,1,0:T(8,128)S(1)}, u32[]{:S(2)}, u32[]{:S(2)}) collective-permute-start(f32[4,32,128]{2,1,0:T(8,128)S(1)} %get-tuple-element.33), channel_id=1, source_target_pairs={{0,3},{1,2},{2,1},{3,0},{4,7},{5,6},{6,5},{7,4},{8,11},{9,10},{10,... | collective-permute-start | bytes 196616 | tf_op jit(solution)/shard_map/ppermute | solution.py:347
  101.1 2.9 %collective-permute-start.21 = (f32[4,32,128]{2,1,0:T(8,128)S(1)}, f32[4,32,128]{2,1,0:T(8,128)S(1)}, u32[]{:S(2)}, u32[]{:S(2)}) collective-permute-start(f32[4,32,128]{2,1,0:T(8,128)S(1)} %get-tuple-element.35), channel_id=1, source_target_pairs={{0,2},{1,3},{2,0},{3,1},{4,6},{5,7},{6,4},{7,5},{8,10},{9,11},{10,... | collective-permute-start | bytes 196616 | tf_op jit(solution)/shard_map/ppermute | solution.py:347
  104.1 0.7 collective-permute-done.20
  104.8 3.2 %collective-permute-done.21 = f32[4,32,128]{2,1,0:T(8,128)S(1)} collective-permute-done((f32[4,32,128]{2,1,0:T(8,128)S(1)}, f32[4,32,128]{2,1,0:T(8,128)S(1)}, u32[]{:S(2)}, u32[]{:S(2)}) %collective-permute-start.21) | collective-permute-done | bytes 65568 | tf_op jit(solution)/shard_map/ppermute | solution.py:347
  108.0 0.7 collective-permute-done.22
  108.7 0.6 add_add_fusion
  (37 shorter events, 2.1 us)
Async XLA Ops:
  5.8 13.6 %collective-permute-start.1 = (f32[5,3,32,128]{3,2,1,0:T(8,128)S(1)}, f32[5,3,32,128]{3,2,1,0:T(8,128)S(1)}, u32[]{:S(2)}, u32[]{:S(2)}) collective-permute-start(f32[5,3,32,128]{3,2,1,0:T(8,128)S(1)} %get-tuple-element.17), channel_id=1, source_target_pairs={{0,1},{1,0},{2,3},{3,2},{4,5},{5,4},{6,7},{7,6},{8,9},{9,8},{10,11... | collective-permute-start | bytes 737288 | tf_op jit(solution)/shard_map/ppermute | solution.py:347
  8.9 24.5 %collective-permute-start.2 = (f32[5,3,32,128]{3,2,1,0:T(8,128)S(1)}, f32[5,3,32,128]{3,2,1,0:T(8,128)S(1)}, u32[]{:S(2)}, u32[]{:S(2)}) collective-permute-start(f32[5,3,32,128]{3,2,1,0:T(8,128)S(1)} %get-tuple-element.18), channel_id=1, source_target_pairs={{0,2},{1,3},{2,0},{3,1},{4,6},{5,7},{6,4},{7,5},{8,10},{9,11},{10,... | collective-permute-start | bytes 737288 | tf_op jit(solution)/shard_map/ppermute | solution.py:347
  11.5 22.1 %collective-permute-start.3 = (f32[5,3,32,128]{3,2,1,0:T(8,128)S(1)}, f32[5,3,32,128]{3,2,1,0:T(8,128)S(1)}, u32[]{:S(2)}, u32[]{:S(2)}) collective-permute-start(f32[5,3,32,128]{3,2,1,0:T(8,128)S(1)} %get-tuple-element.19), channel_id=1, source_target_pairs={{0,3},{1,2},{2,1},{3,0},{4,7},{5,6},{6,5},{7,4},{8,11},{9,10},{10,... | collective-permute-start | bytes 737288 | tf_op jit(solution)/shard_map/ppermute | solution.py:347
  12.2 28.1 %collective-permute-start.4 = (f32[4,3,32,128]{3,2,1,0:T(8,128)}, f32[4,3,32,128]{3,2,1,0:T(8,128)S(1)}, u32[]{:S(2)}, u32[]{:S(2)}) collective-permute-start(f32[4,3,32,128]{3,2,1,0:T(8,128)} %slice.40), channel_id=1, source_target_pairs={{0,28},{4,0},{8,4},{12,8},{16,12},{20,16},{24,20},{28,24},{1,29},{... | collective-permute-start | bytes 589832 | tf_op jit(solution)/shard_map/ppermute | solution.py:343
  13.5 26.8 %collective-permute-start.10 = (f32[4,3,32,128]{3,2,1,0:T(8,128)S(1)}, f32[4,3,32,128]{3,2,1,0:T(8,128)S(1)}, u32[]{:S(2)}, u32[]{:S(2)}) collective-permute-start(f32[4,3,32,128]{3,2,1,0:T(8,128)S(1)} %get-tuple-element.23), channel_id=1, source_target_pairs={{0,3},{1,2},{2,1},{3,0},{4,7},{5,6},{6,5},{7,4},{8,11},{9,10},{10,... | collective-permute-start | bytes 589832 | tf_op jit(solution)/shard_map/ppermute | solution.py:347
  19.4 23.5 %collective-permute-start.8 = (f32[4,3,32,128]{3,2,1,0:T(8,128)S(1)}, f32[4,3,32,128]{3,2,1,0:T(8,128)S(1)}, u32[]{:S(2)}, u32[]{:S(2)}) collective-permute-start(f32[4,3,32,128]{3,2,1,0:T(8,128)S(1)} %get-tuple-element.21), channel_id=1, source_target_pairs={{0,1},{1,0},{2,3},{3,2},{4,5},{5,4},{6,7},{7,6},{8,9},{9,8},{10,11... | collective-permute-start | bytes 589832 | tf_op jit(solution)/shard_map/ppermute | solution.py:347
  33.4 17.3 %collective-permute-start = (f32[8,3,32,128]{3,2,1,0:T(8,128)S(1)}, f32[8,3,32,128]{3,2,1,0:T(8,128)S(1)}, u32[]{:S(2)}, u32[]{:S(2)}) collective-permute-start(f32[8,3,32,128]{3,2,1,0:T(8,128)S(1)} %own_chunk.1.refs_0_), channel_id=1, source_target_pairs={{0,28},{4,0},{8,4},{12,8},{16,12},{20,16},{24,20},{28,24},{1,29},{... | collective-permute-start | bytes 1179656 | tf_op jit(solution)/shard_map/ppermute | solution.py:343
  33.5 16.4 %collective-permute-start.9 = (f32[4,3,32,128]{3,2,1,0:T(8,128)S(1)}, f32[4,3,32,128]{3,2,1,0:T(8,128)S(1)}, u32[]{:S(2)}, u32[]{:S(2)}) collective-permute-start(f32[4,3,32,128]{3,2,1,0:T(8,128)S(1)} %get-tuple-element.22), channel_id=1, source_target_pairs={{0,2},{1,3},{2,0},{3,1},{4,6},{5,7},{6,4},{7,5},{8,10},{9,11},{10,... | collective-permute-start | bytes 589832 | tf_op jit(solution)/shard_map/ppermute | solution.py:347
  40.3 12.2 %collective-permute-start.5 = (f32[4,3,32,128]{3,2,1,0:T(8,128)S(1)}, f32[4,3,32,128]{3,2,1,0:T(8,128)S(1)}, u32[]{:S(2)}, u32[]{:S(2)}) collective-permute-start(f32[4,3,32,128]{3,2,1,0:T(8,128)S(1)} %slice.52), channel_id=1, source_target_pairs={{0,28},{4,0},{8,4},{12,8},{16,12},{20,16},{24,20},{28,24},{1,29},{... | collective-permute-start | bytes 589832 | tf_op jit(solution)/shard_map/ppermute | solution.py:343
  40.3 12.2 %collective-permute-start.6 = (f32[4,3,32,128]{3,2,1,0:T(8,128)S(1)}, f32[4,3,32,128]{3,2,1,0:T(8,128)S(1)}, u32[]{:S(2)}, u32[]{:S(2)}) collective-permute-start(f32[4,3,32,128]{3,2,1,0:T(8,128)S(1)} %slice.53), channel_id=1, source_target_pairs={{0,28},{4,0},{8,4},{12,8},{16,12},{20,16},{24,20},{28,24},{1,29},{... | collective-permute-start | bytes 589832 | tf_op jit(solution)/shard_map/ppermute | solution.py:343
  42.9 10.3 %collective-permute-start.7 = (f32[4,3,32,128]{3,2,1,0:T(8,128)S(1)}, f32[4,3,32,128]{3,2,1,0:T(8,128)S(1)}, u32[]{:S(2)}, u32[]{:S(2)}) collective-permute-start(f32[4,3,32,128]{3,2,1,0:T(8,128)S(1)} %slice.54), channel_id=1, source_target_pairs={{0,28},{4,0},{8,4},{12,8},{16,12},{20,16},{24,20},{28,24},{1,29},{... | collective-permute-start | bytes 589832 | tf_op jit(solution)/shard_map/ppermute | solution.py:343
  49.9 22.5 %collective-permute-start.11 = (f32[4,3,32,128]{3,2,1,0:T(8,128)S(1)}, f32[4,3,32,128]{3,2,1,0:T(8,128)S(1)}, u32[]{:S(2)}, u32[]{:S(2)}) collective-permute-start(f32[4,3,32,128]{3,2,1,0:T(8,128)S(1)} %get-tuple-element.20.refs_6_.refs_3_), channel_id=1, source_target_pairs={{0,28},{4,0},{8,4},{12,8},{16,12},{20,16},{24,20},{28,24},{1,29},{... | collective-permute-start | bytes 589832 | tf_op jit(solution)/shard_map/ppermute | solution.py:343
  50.7 21.7 %collective-permute-start.12 = (f32[4,3,32,128]{3,2,1,0:T(8,128)S(1)}, f32[4,3,32,128]{3,2,1,0:T(8,128)S(1)}, u32[]{:S(2)}, u32[]{:S(2)}) collective-permute-start(f32[4,3,32,128]{3,2,1,0:T(8,128)S(1)} %collective-permute-done.8.refs_7_.refs_4_), channel_id=1, source_target_pairs={{0,28},{4,0},{8,4},{12,8},{16,12},{20,16},{24,20},{28,24},{1,29},{... | collective-permute-start | bytes 589832 | tf_op jit(solution)/shard_map/ppermute | solution.py:343
  52.5 19.9 %collective-permute-start.13 = (f32[4,3,32,128]{3,2,1,0:T(8,128)S(1)}, f32[4,3,32,128]{3,2,1,0:T(8,128)S(1)}, u32[]{:S(2)}, u32[]{:S(2)}) collective-permute-start(f32[4,3,32,128]{3,2,1,0:T(8,128)S(1)} %collective-permute-done.9.refs_8_.refs_5_), channel_id=1, source_target_pairs={{0,28},{4,0},{8,4},{12,8},{16,12},{20,16},{24,20},{28,24},{1,29},{... | collective-permute-start | bytes 589832 | tf_op jit(solution)/shard_map/ppermute | solution.py:343
  52.6 19.9 %collective-permute-start.14 = (f32[4,3,32,128]{3,2,1,0:T(8,128)S(1)}, f32[4,3,32,128]{3,2,1,0:T(8,128)S(1)}, u32[]{:S(2)}, u32[]{:S(2)}) collective-permute-start(f32[4,3,32,128]{3,2,1,0:T(8,128)S(1)} %collective-permute-done.10.refs_9_.refs_6_), channel_id=1, source_target_pairs={{0,28},{4,0},{8,4},{12,8},{16,12},{20,16},{24,20},{28,24},{1,29},{... | collective-permute-start | bytes 589832 | tf_op jit(solution)/shard_map/ppermute | solution.py:343
  78.5 4.6 %collective-permute-start.15 = (f32[2,4,128,128]{3,2,1,0:T(8,128)S(1)}, f32[2,4,128,128]{3,2,1,0:T(8,128)S(1)}, u32[]{:S(2)}, u32[]{:S(2)}) collective-permute-start(f32[2,4,128,128]{3,2,1,0:T(8,128)S(1)} %bitcast.43), channel_id=1, source_target_pairs={{0,4},{4,0},{8,12},{12,8},{16,20},{20,16},{24,28},{28,24},{1,5},{5... | collective-permute-start | bytes 1572872 | tf_op jit(solution)/shard_map/ppermute | solution.py:347
  78.6 6.0 %collective-permute-start.17 = (f32[2,4,128,128]{3,2,1,0:T(8,128)S(1)}, f32[2,4,128,128]{3,2,1,0:T(8,128)S(1)}, u32[]{:S(2)}, u32[]{:S(2)}) collective-permute-start(f32[2,4,128,128]{3,2,1,0:T(8,128)S(1)} %bitcast.44), channel_id=1, source_target_pairs={{0,4},{4,0},{8,12},{12,8},{16,20},{20,16},{24,28},{28,24},{1,5},{5... | collective-permute-start | bytes 1572872 | tf_op jit(solution)/shard_map/ppermute | solution.py:347
  83.1 9.2 %collective-permute-start.16 = (f32[4,128,128]{2,1,0:T(8,128)S(1)}, f32[4,128,128]{2,1,0:T(8,128)S(1)}, u32[]{:S(2)}, u32[]{:S(2)}) collective-permute-start(f32[4,128,128]{2,1,0:T(8,128)S(1)} %fusion.2), channel_id=1, source_target_pairs={{0,8},{4,12},{8,0},{12,4},{16,24},{20,28},{24,16},{28,20},{1,9},{5... | collective-permute-start | bytes 786440 | tf_op jit(solution)/shard_map/ppermute | solution.py:347
  84.7 13.7 %collective-permute-start.18 = (f32[4,128,128]{2,1,0:T(8,128)S(1)}, f32[4,128,128]{2,1,0:T(8,128)S(1)}, u32[]{:S(2)}, u32[]{:S(2)}) collective-permute-start(f32[4,128,128]{2,1,0:T(8,128)S(1)} %get-tuple-element.29), channel_id=1, source_target_pairs={{0,16},{4,20},{8,24},{12,28},{16,0},{20,4},{24,8},{28,12},{1,17},{... | collective-permute-start | bytes 786440 | tf_op jit(solution)/shard_map/ppermute | solution.py:347
  85.3 13.1 %collective-permute-start.19 = (f32[4,128,128]{2,1,0:T(8,128)S(1)}, f32[4,128,128]{2,1,0:T(8,128)S(1)}, u32[]{:S(2)}, u32[]{:S(2)}) collective-permute-start(f32[4,128,128]{2,1,0:T(8,128)S(1)} %get-tuple-element.30), channel_id=1, source_target_pairs={{0,24},{4,28},{8,16},{12,20},{16,8},{20,12},{24,0},{28,4},{1,25},{... | collective-permute-start | bytes 786440 | tf_op jit(solution)/shard_map/ppermute | solution.py:347
  98.5 6.2 %collective-permute-start.20 = (f32[4,32,128]{2,1,0:T(8,128)S(1)}, f32[4,32,128]{2,1,0:T(8,128)S(1)}, u32[]{:S(2)}, u32[]{:S(2)}) collective-permute-start(f32[4,32,128]{2,1,0:T(8,128)S(1)} %get-tuple-element.33), channel_id=1, source_target_pairs={{0,3},{1,2},{2,1},{3,0},{4,7},{5,6},{6,5},{7,4},{8,11},{9,10},{10,... | collective-permute-start | bytes 196616 | tf_op jit(solution)/shard_map/ppermute | solution.py:347
  101.1 6.9 %collective-permute-start.21 = (f32[4,32,128]{2,1,0:T(8,128)S(1)}, f32[4,32,128]{2,1,0:T(8,128)S(1)}, u32[]{:S(2)}, u32[]{:S(2)}) collective-permute-start(f32[4,32,128]{2,1,0:T(8,128)S(1)} %get-tuple-element.35), channel_id=1, source_target_pairs={{0,2},{1,3},{2,0},{3,1},{4,6},{5,7},{6,4},{7,5},{8,10},{9,11},{10,... | collective-permute-start | bytes 196616 | tf_op jit(solution)/shard_map/ppermute | solution.py:347
  104.0 4.7 %collective-permute-start.22 = (f32[4,32,128]{2,1,0:T(8,128)S(1)}, f32[4,32,128]{2,1,0:T(8,128)S(1)}, u32[]{:S(2)}, u32[]{:S(2)}) collective-permute-start(f32[4,32,128]{2,1,0:T(8,128)S(1)} %get-tuple-element.34), channel_id=1, source_target_pairs={{0,1},{1,0},{2,3},{3,2},{4,5},{5,4},{6,7},{7,6},{8,9},{9,8},{10,11... | collective-permute-start | bytes 196616 | tf_op jit(solution)/shard_map/ppermute | solution.py:347

commit v4 on v3

--- a/solution.py
+++ b/solution.py
@@ -30,6 +30,7 @@
     count, nz, rows, nx, chunk, parts = dims
     tiles = nx // LANES
     outs, scratch, hold, in_sems = refs[:-3], refs[-3], refs[-2], refs[-1]
+    edged = any(halos for _, halos in stages)
     depth = nz * tiles * rows
     pitch = depth + PITCH_PAD
 
@@ -62,6 +63,8 @@
                     value = jnp.where(mine, moved(lines[part * chunk // LANES][y], y * chunk - offset), value)
                 hold[part, z] = value
                 after, before = (part + 1) % parts, (part - 1) % parts
+                if not edged:
+                    continue
                 back = moved(value, 4 * z - chunk)
                 on = back if 2 * chunk % LANES == 0 else moved(value, 4 * z + chunk)
                 packed[after] = jnp.where(lows[z], back, packed[after])
@@ -195,13 +198,14 @@
     parts, count, nz, chunk, group, span, xs, ys, zs, has_run, scale, tables = plan
     total = parts * count
     near = {(z + step) % nz for z in zs for step in range(-2, 3)}
-    stages = sorted({z // span for z in near | set(xs + ys)} | ({0} if xs else set()))
+    stages = sorted({z // span for z in near | set(xs + ys)})
     next_stages = sorted({z // span for z in ys})
     refs = list(refs)
     test_ref = refs.pop(0)
     next_test_ref = refs.pop(0) if ys else None
     run_ref = refs.pop(0) if has_run else None
     if tables != "given":
+        edges = [refs.pop(0) for _ in range(parts)] if xs else None
         fields = {stage: [refs.pop(0) for _ in range(parts)] for stage in stages}
         nexts = {stage: [refs.pop(0) for _ in range(parts)] for stage in next_stages}
     if tables == "keep":
@@ -218,7 +222,7 @@
         return pl.ds(pl.multiple_of((me_ref[0] ^ shift) * count, count), count)
 
     def prepare_x():
-        packed = jnp.concatenate([fields[0][shift][span].reshape(3 * count, LANES) for shift in range(parts)], 0)
+        packed = jnp.concatenate([edges[shift][0].reshape(3 * count, LANES) for shift in range(parts)], 0)
         for slab, z in enumerate(xs):
             values = [fields[z // span][shift][z % span].reshape(3 * count, LANES) for shift in range(parts)]
             grads = x_grads(jnp.concatenate(values, 0), packed, z, chunk)
@@ -376,10 +380,13 @@
 def exchange(test_modes, modes, plain, place, levels, dims, scale):
     parts, count, nz, _, group, span = dims
     total, slabs = parts * count, test_modes.shape[0] // group
-    fields = spread(modes, plain, parts, tuple((levels[stage], stage == 0) for stage in range(STAGES)))
+    fields = spread(modes, plain, parts, tuple((levels[stage], False) for stage in range(STAGES)))
     for stage in range(STAGES):
         for other in range(parts - 1, 0, -1):
             fields[stage][other] = swapped_with(fields[stage][other], "mode", other)
+    edges = spread(modes, plain, parts, (((), True),))[0]
+    for other in range(parts - 1, 0, -1):
+        edges[other] = swapped_with(edges[other], "mode", other)
     test = own_chunk(test_modes, plain, parts)
     next_test = shifted(test, "space", -1)
     nexts = []
@@ -389,14 +396,14 @@
     running = None
     for stage in range(STAGES - 1):
         for kind in ("x", "y"):
-            held = fields[stage] if stage == 0 or kind == "y" else fields[0] + fields[stage]
+            held = fields[stage]
             plan = dims + ((levels[stage], (), ()) if kind == "x" else ((), levels[stage], ()))
             plan += (running is not None, None, "")
             given = [test] + ([next_test] if kind == "y" else []) + ([running] if running is not None else [])
-            given += held + nexts[stage] if kind == "y" else held
+            given += held + nexts[stage] if kind == "y" else edges + held
             running = part_call(plan, plain, slabs, given, running)[0]
     plan = dims + (levels[-1], (), tuple(range(nz)), running is not None, None, "")
-    given = [test] + ([running] if running is not None else []) + sum(fields, [])
+    given = [test] + ([running] if running is not None else []) + edges + sum(fields, [])
     running = part_call(plan, plain, slabs, given, running)[0]
 
     me = plain[0]

time: 109 us -> 107 us (0.982)
  waiting for transfers between devices: 32.4 us -> 29.7 us
  Pallas kernels: 41.9 us -> 44.2 us
  starting transfers between devices: 32.9 us -> 31.6 us
    ppermute x14 -> x17, waiting for transfers between devices: 32.4 us -> 29.7 us  [swapped_with(): lax.ppermute(value, axis, [(i, i ^ other) for i in range(lax.axis_size(ax...]
    pallas_call x1 -> x2, Pallas kernels: 5.67 us -> 7.91 us  [spread(): pl.pallas_call(partial(spread_kernel, dims, stages), out_shape=[pltpu.VME...]
    ppermute x14 -> x17, starting transfers between devices: 25.7 us -> 24.5 us  [swapped_with(): lax.ppermute(value, axis, [(i, i ^ other) for i in range(lax.axis_size(ax...]
  transfers between devices with their start and end apart: 23 -> 26, of which waited for: 8 -> 8; matrix products, arithmetic and copies ran while one was open for 1% -> 0% of each run, Pallas kernels for 28% -> 34%
where the time goes in v4:
time: 107 us
  Pallas kernels  44.2 us (41%)
  starting transfers between devices  31.6 us (30%)
  waiting for transfers between devices  29.7 us (28%)
    pallas_call x7, Pallas kernels, part_call(): pl.pallas_call(partial(part_kernel, plan, steps), in_specs=[pl.BlockSpec(...  34 us
    ppermute x17, waiting for transfers between devices, swapped_with(): lax.ppermute(value, axis, [(i, i ^ other) for i in range(lax.axis_size(ax...  29.7 us
    ppermute x17, starting transfers between devices, swapped_with(): lax.ppermute(value, axis, [(i, i ^ other) for i in range(lax.axis_size(ax...  24.5 us
    pallas_call x2, Pallas kernels, spread(): pl.pallas_call(partial(spread_kernel, dims, stages), out_shape=[pltpu.VME...  7.91 us
    ppermute x9, starting transfers between devices, shifted(): lax.ppermute(value, axis, [(i, (i + shift) % size) for i in range(size)])  7.13 us
    pallas_call x1, Pallas kernels, own_chunk(): pl.pallas_call(partial(own_kernel, (count, nz, rows, nx, nx // parts)), o...  2.23 us
  transfers between devices with their start and end apart: 26, of which 8 were waited for; matrix products, arithmetic and copies ran while one was open for 0% of the time, Pallas kernels for 34%

profile of v4, /device:TPU:0, one launch (start us, length us, event | category | flops | bytes accessed | tf_op | source)
XLA Modules:
  0.0 106.8 jit_solution(5721120126866340736)
XLA Ops:
  0.1 2.3 %spread.3 = (f32[4,3,32,128]{3,2,1,0:T(8,128)S(1)}, f32[4,3,32,128]{3,2,1,0:T(8,128)S(1)}, f32[4,3,32,128]{3,2,1,0:T(8,128)S(1)}, f32[4,3,32,128]{3,2,1,0:T(8,12...) custom-call(s32[4]{0:T(128)S(1)} %pad_add_fusion.2.me_ref, ...), custom_call_target="tpu_custom_call" | custom-call | tf_op jit(solution)/shard_map/spread/pallas_call | solution.py:101
  2.4 3.1 %collective-permute-start.4 = (f32[4,3,32,128]{3,2,1,0:T(8,128)S(1)}, f32[4,3,32,128]{3,2,1,0:T(8,128)S(1)}, u32[]{:S(2)}, u32[]{:S(2)}) collective-permute-start(f32[4,3,32,128]{3,2,1,0:T(8,128)S(1)} %get-tuple-element.25), channel_id=1, source_target_pairs={{0,1},{1,0},{2,3},{3,2},{4,5},{5,4},{6,7},{7,6},{8,9},{9,8},{10,11... | collective-permute-start | bytes 589832 | tf_op jit(solution)/shard_map/ppermute | solution.py:351
  5.5 2.6 %collective-permute-start.5 = (f32[4,3,32,128]{3,2,1,0:T(8,128)S(1)}, f32[4,3,32,128]{3,2,1,0:T(8,128)S(1)}, u32[]{:S(2)}, u32[]{:S(2)}) collective-permute-start(f32[4,3,32,128]{3,2,1,0:T(8,128)S(1)} %get-tuple-element.26), channel_id=1, source_target_pairs={{0,2},{1,3},{2,0},{3,1},{4,6},{5,7},{6,4},{7,5},{8,10},{9,11},{10,... | collective-permute-start | bytes 589832 | tf_op jit(solution)/shard_map/ppermute | solution.py:351
  8.1 5.6 %spread.2 = (f32[1,3,32,128]{3,2,1,0:T(8,128)S(1)}, f32[1,3,32,128]{3,2,1,0:T(8,128)S(1)}, f32[1,3,32,128]{3,2,1,0:T(8,128)S(1)}, f32[1,3,32,128]{3,2,1,0:T(8,128)S(1)}) custom-call(s32[4]{0:T(128)S(1)} %pad_add_fusion.2.me_ref, f32[32,96,128]{2,1,0:T(8,128)} %bitcast.46), custom_call_target="tpu_custom_call" | custom-call | tf_op jit(solution)/shard_map/spread/pallas_call | solution.py:101
  13.7 0.5 collective-permute-start.1
  14.2 3.9 %collective-permute-start.3 = (f32[1,3,32,128]{3,2,1,0:T(8,128)S(1)}, f32[1,3,32,128]{3,2,1,0:T(8,128)S(1)}, u32[]{:S(2)}, u32[]{:S(2)}) collective-permute-start(f32[1,3,32,128]{3,2,1,0:T(8,128)S(1)} %get-tuple-element.23), channel_id=1, source_target_pairs={{0,3},{1,2},{2,1},{3,0},{4,7},{5,6},{6,5},{7,4},{8,11},{9,10},{10,... | collective-permute-start | bytes 147464 | tf_op jit(solution)/shard_map/ppermute | solution.py:351
  18.4 4.8 %collective-permute-done.2.refs_3_.refs_4_ = f32[1,3,32,128]{3,2,1,0:T(8,128)S(1)} collective-permute-done((f32[1,3,32,128]{3,2,1,0:T(8,128)S(1)}, f32[1,3,32,128]{3,2,1,0:T(8,128)S(1)}, u32[]{:S(2)}, u32[]{:S(2)}) %collective-permute-start.2) | collective-permute-done | bytes 49184 | tf_op jit(solution)/shard_map/ppermute | solution.py:351
  23.2 3.7 %collective-permute-start.11 = (f32[4,3,32,128]{3,2,1,0:T(8,128)S(1)}, f32[4,3,32,128]{3,2,1,0:T(8,128)S(1)}, u32[]{:S(2)}, u32[]{:S(2)}) collective-permute-start(f32[4,3,32,128]{3,2,1,0:T(8,128)S(1)} %get-tuple-element.29), channel_id=1, source_target_pairs={{0,1},{1,0},{2,3},{3,2},{4,5},{5,4},{6,7},{7,6},{8,9},{9,8},{10,11... | collective-permute-start | bytes 589832 | tf_op jit(solution)/shard_map/ppermute | solution.py:351
  26.9 1.8 %collective-permute-start.12 = (f32[4,3,32,128]{3,2,1,0:T(8,128)S(1)}, f32[4,3,32,128]{3,2,1,0:T(8,128)S(1)}, u32[]{:S(2)}, u32[]{:S(2)}) collective-permute-start(f32[4,3,32,128]{3,2,1,0:T(8,128)S(1)} %get-tuple-element.30), channel_id=1, source_target_pairs={{0,2},{1,3},{2,0},{3,1},{4,6},{5,7},{6,4},{7,5},{8,10},{9,11},{10,... | collective-permute-start | bytes 589832 | tf_op jit(solution)/shard_map/ppermute | solution.py:351
  28.7 2.2 %own_chunk.1.refs_0_ = f32[8,3,32,128]{3,2,1,0:T(8,128)S(1)} custom-call(s32[4]{0:T(128)S(1)} %pad_add_fusion.2.me_ref, f32[32,96,128]{2,1,0:T(8,128)} %bitcast.47), custom_call_target="tpu_custom_call" | custom-call | tf_op jit(solution)/shard_map/own_chunk/pallas_call | solution.py:141
  30.9 2.0 %collective-permute-start = (f32[8,3,32,128]{3,2,1,0:T(8,128)S(1)}, f32[8,3,32,128]{3,2,1,0:T(8,128)S(1)}, u32[]{:S(2)}, u32[]{:S(2)}) collective-permute-start(f32[8,3,32,128]{3,2,1,0:T(8,128)S(1)} %own_chunk.1.refs_0_), channel_id=1, source_target_pairs={{0,28},{4,0},{8,4},{12,8},{16,12},{20,16},{24,20},{28,24},{1,29},{... | collective-permute-start | bytes 1179656 | tf_op jit(solution)/shard_map/ppermute | solution.py:347
  33.2 1.3 %collective-permute-start.10 = (f32[4,3,32,128]{3,2,1,0:T(8,128)S(1)}, f32[4,3,32,128]{3,2,1,0:T(8,128)S(1)}, u32[]{:S(2)}, u32[]{:S(2)}) collective-permute-start(f32[4,3,32,128]{3,2,1,0:T(8,128)S(1)} %collective-permute-done.6.refs_8_.refs_6_.refs_9_), channel_id=1, source_target_pairs={{0,28},{4,0},{8,4},{12,8},{16,12},{20,16},{24,20},{28,24},{1,29},{... | collective-permute-start | bytes 589832 | tf_op jit(solution)/shard_map/ppermute | solution.py:347
  34.7 8.7 %collective-permute-done.12.refs_12_.refs_5_ = f32[4,3,32,128]{3,2,1,0:T(8,128)S(1)} collective-permute-done((f32[4,3,32,128]{3,2,1,0:T(8,128)S(1)}, f32[4,3,32,128]{3,2,1,0:T(8,128)S(1)}, u32[]{:S(2)}, u32[]{:S(2)}) %collective-permute-start.12) | collective-permute-done | bytes 196640 | tf_op jit(solution)/shard_map/ppermute | solution.py:351
  43.5 4.9 %shard_map.28.refs_2_ = f32[4096,128]{1,0:T(8,128)S(1)} custom-call(s32[4]{0:T(128)S(1)} %pad_add_fusion.2.me_ref, f32[8,3,32,128]{3,2,1,0:T(8,128)S(1)} %own_chunk.1.refs_0_, f32[1,3,32,128]{3,2,1,0:T(8,128)S(1)} %get-tuple-element.20.refs_1_.refs_2_, f32[1,3,32,128]{3,2,1,0:T(8,128)S(1)} %collective-permute-done.1.refs_2_.refs_3_, ...), custom_call_target="tpu_custom_call" | custom-call | flops 1610612736 | bytes 4194304 | tf_op jit(solution)/shard_map/pallas_call | solution.py:331
  48.3 2.6 %collective-permute-start.14 = (f32[4,3,32,128]{3,2,1,0:T(8,128)S(1)}, f32[4,3,32,128]{3,2,1,0:T(8,128)S(1)}, u32[]{:S(2)}, u32[]{:S(2)}) collective-permute-start(f32[4,3,32,128]{3,2,1,0:T(8,128)S(1)} %get-tuple-element.28.refs_10_.refs_3_), channel_id=1, source_target_pairs={{0,28},{4,0},{8,4},{12,8},{16,12},{20,16},{24,20},{28,24},{1,29},{... | collective-permute-start | bytes 589832 | tf_op jit(solution)/shard_map/ppermute | solution.py:347
  51.0 0.6 collective-permute-start.16
  51.9 8.3 %shard_map.29.refs_1_ = f32[4096,128]{1,0:T(8,128)S(1)} custom-call(s32[4]{0:T(128)S(1)} %pad_add_fusion.2.me_ref, f32[8,3,32,128]{3,2,1,0:T(8,128)S(1)} %own_chunk.1.refs_0_, f32[8,3,32,128]{3,2,1,0:T(8,128)S(1)} %collective-permute-done.refs_1_, f32[4096,128]{1,0:T(8,128)S(1)} %shard_map.28.refs_2_, ...), custom_call_target="tpu_custom_call", output_to_operand_aliasing={{}: (3, {})} | custom-call | flops 3221225472 | bytes 4194304 | tf_op jit(solution)/shard_map/pallas_call | solution.py:331
  60.1 11.0 %shard_map.30.refs_2_ = f32[4096,128]{1,0:T(8,128)S(1)} custom-call(s32[4]{0:T(128)S(1)} %pad_add_fusion.2.me_ref, f32[8,3,32,128]{3,2,1,0:T(8,128)S(1)} %own_chunk.1.refs_0_, f32[4096,128]{1,0:T(8,128)S(1)} %shard_map.29.refs_1_, f32[1,3,32,128]{3,2,1,0:T(8,128)S(1)} %get-tuple-element.20.refs_1_.refs_2_, ...), custom_call_target="tpu_custom_call", output_to_operand_aliasing={{}: (2, {})} | custom-call | flops 4831838208 | bytes 4194304 | tf_op jit(solution)/shard_map/pallas_call | solution.py:331
  71.1 4.1 %shard_map.31 = (f32[1024,128]{1,0:T(8,128)S(1)}, f32[24,128,128]{2,1,0:T(8,128)S(1)}, bf16[1024,256]{1,0:T(8,128)(2,1)S(1)}) custom-call(s32[4]{0:T(128)S(1)} %get-tuple-element.47.me_ref, f32[8,3,32,128]{3,2,1,0:T(8,128)S(1)} %own_chunk.1.refs_0_, f32[8,3,32,128]{3,2,1,0:T(8,128)S(1)} %collective-permute-done.refs_1_, f32[4096,128]{1,0:T(8,128)S(1)} %shard_map.30.refs_2_, ...), custom_call_target="tpu_custom_call" | custom-call | flops 805306368 | bytes 1048576 | tf_op jit(solution)/shard_map/pallas_call | solution.py:331
  75.2 2.0 %shard_map.33 = f32[1024,128]{1,0:T(8,128)S(1)} custom-call(s32[4]{0:T(128)S(1)} %get-tuple-element.44.me_ref, f32[8,3,32,128]{3,2,1,0:T(8,128)S(1)} %own_chunk.1.refs_0_, f32[8,3,32,128]{3,2,1,0:T(8,128)S(1)} %collective-permute-done.refs_1_, f32[4096,128]{1,0:T(8,128)S(1)} %shard_map.30.refs_2_, f32[24,128,128]{2,1,0:T(8,128)S(1)} %get-tuple-element.32.refs_3_, ...), custom_call_target="tpu_custom_call" | custom-call | flops 805306368 | bytes 1048576 | tf_op jit(solution)/shard_map/pallas_call | solution.py:331
  77.7 2.0 %shard_map.32 = f32[1024,128]{1,0:T(8,128)S(1)} custom-call(s32[4]{0:T(128)S(1)} %get-tuple-element.45.me_ref, f32[8,3,32,128]{3,2,1,0:T(8,128)S(1)} %own_chunk.1.refs_0_, f32[8,3,32,128]{3,2,1,0:T(8,128)S(1)} %collective-permute-done.refs_1_, f32[4096,128]{1,0:T(8,128)S(1)} %shard_map.30.refs_2_, f32[24,128,128]{2,1,0:T(8,128)S(1)} %get-tuple-element.32.refs_3_, ...), custom_call_target="tpu_custom_call" | custom-call | flops 805306368 | bytes 1048576 | tf_op jit(solution)/shard_map/pallas_call | solution.py:331
  79.7 2.0 %shard_map.34 = f32[1024,128]{1,0:T(8,128)S(1)} custom-call(s32[4]{0:T(128)S(1)} %get-tuple-element.46.me_ref, f32[8,3,32,128]{3,2,1,0:T(8,128)S(1)} %own_chunk.1.refs_0_, f32[8,3,32,128]{3,2,1,0:T(8,128)S(1)} %collective-permute-done.refs_1_, f32[4096,128]{1,0:T(8,128)S(1)} %shard_map.30.refs_2_, f32[24,128,128]{2,1,0:T(8,128)S(1)} %get-tuple-element.32.refs_3_, ...), custom_call_target="tpu_custom_call" | custom-call | flops 805306368 | bytes 1048576 | tf_op jit(solution)/shard_map/pallas_call | solution.py:331
  81.8 1.6 %collective-permute-start.19 = (f32[4,128,128]{2,1,0:T(8,128)S(1)}, f32[4,128,128]{2,1,0:T(8,128)S(1)}, u32[]{:S(2)}, u32[]{:S(2)}) collective-permute-start(f32[4,128,128]{2,1,0:T(8,128)S(1)} %fusion.2), channel_id=1, source_target_pairs={{0,8},{4,12},{8,0},{12,4},{16,24},{20,28},{24,16},{28,20},{1,9},{5... | collective-permute-start | bytes 786440 | tf_op jit(solution)/shard_map/ppermute | solution.py:351
  83.4 0.6 collective-permute-start.21
  84.0 1.5 %collective-permute-start.22 = (f32[4,128,128]{2,1,0:T(8,128)S(1)}, f32[4,128,128]{2,1,0:T(8,128)S(1)}, u32[]{:S(2)}, u32[]{:S(2)}) collective-permute-start(f32[4,128,128]{2,1,0:T(8,128)S(1)} %get-tuple-element.38), channel_id=1, source_target_pairs={{0,24},{4,28},{8,16},{12,20},{16,8},{20,12},{24,0},{28,4},{1,25},{... | collective-permute-start | bytes 786440 | tf_op jit(solution)/shard_map/ppermute | solution.py:351
  85.5 5.5 %collective-permute-done.19 = f32[4,128,128]{2,1,0:T(8,128)S(1)} collective-permute-done((f32[4,128,128]{2,1,0:T(8,128)S(1)}, f32[4,128,128]{2,1,0:T(8,128)S(1)}, u32[]{:S(2)}, u32[]{:S(2)}) %collective-permute-start.19) | collective-permute-done | bytes 262176 | tf_op jit(solution)/shard_map/ppermute | solution.py:351
  91.0 6.3 %collective-permute-done.21 = f32[4,128,128]{2,1,0:T(8,128)S(1)} collective-permute-done((f32[4,128,128]{2,1,0:T(8,128)S(1)}, f32[4,128,128]{2,1,0:T(8,128)S(1)}, u32[]{:S(2)}, u32[]{:S(2)}) %collective-permute-start.21) | collective-permute-done | bytes 262176 | tf_op jit(solution)/shard_map/ppermute | solution.py:351
  97.4 3.1 %collective-permute-start.23 = (f32[4,32,128]{2,1,0:T(8,128)S(1)}, f32[4,32,128]{2,1,0:T(8,128)S(1)}, u32[]{:S(2)}, u32[]{:S(2)}) collective-permute-start(f32[4,32,128]{2,1,0:T(8,128)S(1)} %get-tuple-element.41), channel_id=1, source_target_pairs={{0,3},{1,2},{2,1},{3,0},{4,7},{5,6},{6,5},{7,4},{8,11},{9,10},{10,... | collective-permute-start | bytes 196616 | tf_op jit(solution)/shard_map/ppermute | solution.py:351
  100.5 1.4 %collective-permute-start.25 = (f32[4,32,128]{2,1,0:T(8,128)S(1)}, f32[4,32,128]{2,1,0:T(8,128)S(1)}, u32[]{:S(2)}, u32[]{:S(2)}) collective-permute-start(f32[4,32,128]{2,1,0:T(8,128)S(1)} %get-tuple-element.42), channel_id=1, source_target_pairs={{0,1},{1,0},{2,3},{3,2},{4,5},{5,4},{6,7},{7,6},{8,9},{9,8},{10,11... | collective-permute-start | bytes 196616 | tf_op jit(solution)/shard_map/ppermute | solution.py:351
  101.9 1.7 %collective-permute-done.23 = f32[4,32,128]{2,1,0:T(8,128)S(1)} collective-permute-done((f32[4,32,128]{2,1,0:T(8,128)S(1)}, f32[4,32,128]{2,1,0:T(8,128)S(1)}, u32[]{:S(2)}, u32[]{:S(2)}) %collective-permute-start.23) | collective-permute-done | bytes 65568 | tf_op jit(solution)/shard_map/ppermute | solution.py:351
  103.5 2.2 %collective-permute-done.24 = f32[4,32,128]{2,1,0:T(8,128)S(1)} collective-permute-done((f32[4,32,128]{2,1,0:T(8,128)S(1)}, f32[4,32,128]{2,1,0:T(8,128)S(1)}, u32[]{:S(2)}, u32[]{:S(2)}) %collective-permute-start.24) | collective-permute-done | bytes 65568 | tf_op jit(solution)/shard_map/ppermute | solution.py:351
  106.1 0.6 add_add_fusion
  (40 shorter events, 2.5 us)
Async XLA Ops:
  2.4 24.5 %collective-permute-start.4 = (f32[4,3,32,128]{3,2,1,0:T(8,128)S(1)}, f32[4,3,32,128]{3,2,1,0:T(8,128)S(1)}, u32[]{:S(2)}, u32[]{:S(2)}) collective-permute-start(f32[4,3,32,128]{3,2,1,0:T(8,128)S(1)} %get-tuple-element.25), channel_id=1, source_target_pairs={{0,1},{1,0},{2,3},{3,2},{4,5},{5,4},{6,7},{7,6},{8,9},{9,8},{10,11... | collective-permute-start | bytes 589832 | tf_op jit(solution)/shard_map/ppermute | solution.py:351
  5.5 25.4 %collective-permute-start.5 = (f32[4,3,32,128]{3,2,1,0:T(8,128)S(1)}, f32[4,3,32,128]{3,2,1,0:T(8,128)S(1)}, u32[]{:S(2)}, u32[]{:S(2)}) collective-permute-start(f32[4,3,32,128]{3,2,1,0:T(8,128)S(1)} %get-tuple-element.26), channel_id=1, source_target_pairs={{0,2},{1,3},{2,0},{3,1},{4,6},{5,7},{6,4},{7,5},{8,10},{9,11},{10,... | collective-permute-start | bytes 589832 | tf_op jit(solution)/shard_map/ppermute | solution.py:351
  13.7 4.6 %collective-permute-start.1 = (f32[1,3,32,128]{3,2,1,0:T(8,128)S(1)}, f32[1,3,32,128]{3,2,1,0:T(8,128)S(1)}, u32[]{:S(2)}, u32[]{:S(2)}) collective-permute-start(f32[1,3,32,128]{3,2,1,0:T(8,128)S(1)} %get-tuple-element.21), channel_id=1, source_target_pairs={{0,1},{1,0},{2,3},{3,2},{4,5},{5,4},{6,7},{7,6},{8,9},{9,8},{10,11... | collective-permute-start | bytes 147464 | tf_op jit(solution)/shard_map/ppermute | solution.py:351
  14.2 9.0 %collective-permute-start.2 = (f32[1,3,32,128]{3,2,1,0:T(8,128)S(1)}, f32[1,3,32,128]{3,2,1,0:T(8,128)S(1)}, u32[]{:S(2)}, u32[]{:S(2)}) collective-permute-start(f32[1,3,32,128]{3,2,1,0:T(8,128)S(1)} %get-tuple-element.22), channel_id=1, source_target_pairs={{0,2},{1,3},{2,0},{3,1},{4,6},{5,7},{6,4},{7,5},{8,10},{9,11},{10,... | collective-permute-start | bytes 147464 | tf_op jit(solution)/shard_map/ppermute | solution.py:351
  14.2 9.0 %collective-permute-start.3 = (f32[1,3,32,128]{3,2,1,0:T(8,128)S(1)}, f32[1,3,32,128]{3,2,1,0:T(8,128)S(1)}, u32[]{:S(2)}, u32[]{:S(2)}) collective-permute-start(f32[1,3,32,128]{3,2,1,0:T(8,128)S(1)} %get-tuple-element.23), channel_id=1, source_target_pairs={{0,3},{1,2},{2,1},{3,0},{4,7},{5,6},{6,5},{7,4},{8,11},{9,10},{10,... | collective-permute-start | bytes 147464 | tf_op jit(solution)/shard_map/ppermute | solution.py:351
  18.3 14.7 %collective-permute-start.6 = (f32[4,3,32,128]{3,2,1,0:T(8,128)S(1)}, f32[4,3,32,128]{3,2,1,0:T(8,128)S(1)}, u32[]{:S(2)}, u32[]{:S(2)}) collective-permute-start(f32[4,3,32,128]{3,2,1,0:T(8,128)S(1)} %get-tuple-element.27), channel_id=1, source_target_pairs={{0,3},{1,2},{2,1},{3,0},{4,7},{5,6},{6,5},{7,4},{8,11},{9,10},{10,... | collective-permute-start | bytes 589832 | tf_op jit(solution)/shard_map/ppermute | solution.py:351
  23.2 9.9 %collective-permute-start.7 = (f32[4,3,32,128]{3,2,1,0:T(8,128)S(1)}, f32[4,3,32,128]{3,2,1,0:T(8,128)S(1)}, u32[]{:S(2)}, u32[]{:S(2)}) collective-permute-start(f32[4,3,32,128]{3,2,1,0:T(8,128)S(1)} %get-tuple-element.24.refs_5_.refs_3_.refs_6_), channel_id=1, source_target_pairs={{0,28},{4,0},{8,4},{12,8},{16,12},{20,16},{24,20},{28,24},{1,29},{... | collective-permute-start | bytes 589832 | tf_op jit(solution)/shard_map/ppermute | solution.py:347
  23.2 11.2 %collective-permute-start.11 = (f32[4,3,32,128]{3,2,1,0:T(8,128)S(1)}, f32[4,3,32,128]{3,2,1,0:T(8,128)S(1)}, u32[]{:S(2)}, u32[]{:S(2)}) collective-permute-start(f32[4,3,32,128]{3,2,1,0:T(8,128)S(1)} %get-tuple-element.29), channel_id=1, source_target_pairs={{0,1},{1,0},{2,3},{3,2},{4,5},{5,4},{6,7},{7,6},{8,9},{9,8},{10,11... | collective-permute-start | bytes 589832 | tf_op jit(solution)/shard_map/ppermute | solution.py:351
  26.9 16.5 %collective-permute-start.12 = (f32[4,3,32,128]{3,2,1,0:T(8,128)S(1)}, f32[4,3,32,128]{3,2,1,0:T(8,128)S(1)}, u32[]{:S(2)}, u32[]{:S(2)}) collective-permute-start(f32[4,3,32,128]{3,2,1,0:T(8,128)S(1)} %get-tuple-element.30), channel_id=1, source_target_pairs={{0,2},{1,3},{2,0},{3,1},{4,6},{5,7},{6,4},{7,5},{8,10},{9,11},{10,... | collective-permute-start | bytes 589832 | tf_op jit(solution)/shard_map/ppermute | solution.py:351
  30.9 20.9 %collective-permute-start = (f32[8,3,32,128]{3,2,1,0:T(8,128)S(1)}, f32[8,3,32,128]{3,2,1,0:T(8,128)S(1)}, u32[]{:S(2)}, u32[]{:S(2)}) collective-permute-start(f32[8,3,32,128]{3,2,1,0:T(8,128)S(1)} %own_chunk.1.refs_0_), channel_id=1, source_target_pairs={{0,28},{4,0},{8,4},{12,8},{16,12},{20,16},{24,20},{28,24},{1,29},{... | collective-permute-start | bytes 1179656 | tf_op jit(solution)/shard_map/ppermute | solution.py:347
  33.1 15.3 %collective-permute-start.13 = (f32[4,3,32,128]{3,2,1,0:T(8,128)S(1)}, f32[4,3,32,128]{3,2,1,0:T(8,128)S(1)}, u32[]{:S(2)}, u32[]{:S(2)}) collective-permute-start(f32[4,3,32,128]{3,2,1,0:T(8,128)S(1)} %get-tuple-element.31), channel_id=1, source_target_pairs={{0,3},{1,2},{2,1},{3,0},{4,7},{5,6},{6,5},{7,4},{8,11},{9,10},{10,... | collective-permute-start | bytes 589832 | tf_op jit(solution)/shard_map/ppermute | solution.py:351
  33.2 17.8 %collective-permute-start.10 = (f32[4,3,32,128]{3,2,1,0:T(8,128)S(1)}, f32[4,3,32,128]{3,2,1,0:T(8,128)S(1)}, u32[]{:S(2)}, u32[]{:S(2)}) collective-permute-start(f32[4,3,32,128]{3,2,1,0:T(8,128)S(1)} %collective-permute-done.6.refs_8_.refs_6_.refs_9_), channel_id=1, source_target_pairs={{0,28},{4,0},{8,4},{12,8},{16,12},{20,16},{24,20},{28,24},{1,29},{... | collective-permute-start | bytes 589832 | tf_op jit(solution)/shard_map/ppermute | solution.py:347
  34.4 16.6 %collective-permute-start.8 = (f32[4,3,32,128]{3,2,1,0:T(8,128)S(1)}, f32[4,3,32,128]{3,2,1,0:T(8,128)S(1)}, u32[]{:S(2)}, u32[]{:S(2)}) collective-permute-start(f32[4,3,32,128]{3,2,1,0:T(8,128)S(1)} %collective-permute-done.4.refs_6_.refs_4_.refs_7_), channel_id=1, source_target_pairs={{0,28},{4,0},{8,4},{12,8},{16,12},{20,16},{24,20},{28,24},{1,29},{... | collective-permute-start | bytes 589832 | tf_op jit(solution)/shard_map/ppermute | solution.py:347
  43.4 8.2 %collective-permute-start.9 = (f32[4,3,32,128]{3,2,1,0:T(8,128)S(1)}, f32[4,3,32,128]{3,2,1,0:T(8,128)S(1)}, u32[]{:S(2)}, u32[]{:S(2)}) collective-permute-start(f32[4,3,32,128]{3,2,1,0:T(8,128)S(1)} %collective-permute-done.5.refs_7_.refs_5_.refs_8_), channel_id=1, source_target_pairs={{0,28},{4,0},{8,4},{12,8},{16,12},{20,16},{24,20},{28,24},{1,29},{... | collective-permute-start | bytes 589832 | tf_op jit(solution)/shard_map/ppermute | solution.py:347
  48.3 22.8 %collective-permute-start.14 = (f32[4,3,32,128]{3,2,1,0:T(8,128)S(1)}, f32[4,3,32,128]{3,2,1,0:T(8,128)S(1)}, u32[]{:S(2)}, u32[]{:S(2)}) collective-permute-start(f32[4,3,32,128]{3,2,1,0:T(8,128)S(1)} %get-tuple-element.28.refs_10_.refs_3_), channel_id=1, source_target_pairs={{0,28},{4,0},{8,4},{12,8},{16,12},{20,16},{24,20},{28,24},{1,29},{... | collective-permute-start | bytes 589832 | tf_op jit(solution)/shard_map/ppermute | solution.py:347
  51.0 20.1 %collective-permute-start.15 = (f32[4,3,32,128]{3,2,1,0:T(8,128)S(1)}, f32[4,3,32,128]{3,2,1,0:T(8,128)S(1)}, u32[]{:S(2)}, u32[]{:S(2)}) collective-permute-start(f32[4,3,32,128]{3,2,1,0:T(8,128)S(1)} %collective-permute-done.11.refs_11_.refs_4_), channel_id=1, source_target_pairs={{0,28},{4,0},{8,4},{12,8},{16,12},{20,16},{24,20},{28,24},{1,29},{... | collective-permute-start | bytes 589832 | tf_op jit(solution)/shard_map/ppermute | solution.py:347
  51.0 20.1 %collective-permute-start.16 = (f32[4,3,32,128]{3,2,1,0:T(8,128)S(1)}, f32[4,3,32,128]{3,2,1,0:T(8,128)S(1)}, u32[]{:S(2)}, u32[]{:S(2)}) collective-permute-start(f32[4,3,32,128]{3,2,1,0:T(8,128)S(1)} %collective-permute-done.12.refs_12_.refs_5_), channel_id=1, source_target_pairs={{0,28},{4,0},{8,4},{12,8},{16,12},{20,16},{24,20},{28,24},{1,29},{... | collective-permute-start | bytes 589832 | tf_op jit(solution)/shard_map/ppermute | solution.py:347
  51.6 19.5 %collective-permute-start.17 = (f32[4,3,32,128]{3,2,1,0:T(8,128)S(1)}, f32[4,3,32,128]{3,2,1,0:T(8,128)S(1)}, u32[]{:S(2)}, u32[]{:S(2)}) collective-permute-start(f32[4,3,32,128]{3,2,1,0:T(8,128)S(1)} %collective-permute-done.13.refs_13_.refs_6_), channel_id=1, source_target_pairs={{0,28},{4,0},{8,4},{12,8},{16,12},{20,16},{24,20},{28,24},{1,29},{... | collective-permute-start | bytes 589832 | tf_op jit(solution)/shard_map/ppermute | solution.py:347
  77.2 4.6 %collective-permute-start.18 = (f32[2,4,128,128]{3,2,1,0:T(8,128)S(1)}, f32[2,4,128,128]{3,2,1,0:T(8,128)S(1)}, u32[]{:S(2)}, u32[]{:S(2)}) collective-permute-start(f32[2,4,128,128]{3,2,1,0:T(8,128)S(1)} %bitcast.43), channel_id=1, source_target_pairs={{0,4},{4,0},{8,12},{12,8},{16,20},{20,16},{24,28},{28,24},{1,5},{5... | collective-permute-start | bytes 1572872 | tf_op jit(solution)/shard_map/ppermute | solution.py:351
  77.5 5.9 %collective-permute-start.20 = (f32[2,4,128,128]{3,2,1,0:T(8,128)S(1)}, f32[2,4,128,128]{3,2,1,0:T(8,128)S(1)}, u32[]{:S(2)}, u32[]{:S(2)}) collective-permute-start(f32[2,4,128,128]{3,2,1,0:T(8,128)S(1)} %bitcast.44), channel_id=1, source_target_pairs={{0,4},{4,0},{8,12},{12,8},{16,20},{20,16},{24,28},{28,24},{1,5},{5... | collective-permute-start | bytes 1572872 | tf_op jit(solution)/shard_map/ppermute | solution.py:351
  81.8 9.2 %collective-permute-start.19 = (f32[4,128,128]{2,1,0:T(8,128)S(1)}, f32[4,128,128]{2,1,0:T(8,128)S(1)}, u32[]{:S(2)}, u32[]{:S(2)}) collective-permute-start(f32[4,128,128]{2,1,0:T(8,128)S(1)} %fusion.2), channel_id=1, source_target_pairs={{0,8},{4,12},{8,0},{12,4},{16,24},{20,28},{24,16},{28,20},{1,9},{5... | collective-permute-start | bytes 786440 | tf_op jit(solution)/shard_map/ppermute | solution.py:351
  83.4 13.9 %collective-permute-start.21 = (f32[4,128,128]{2,1,0:T(8,128)S(1)}, f32[4,128,128]{2,1,0:T(8,128)S(1)}, u32[]{:S(2)}, u32[]{:S(2)}) collective-permute-start(f32[4,128,128]{2,1,0:T(8,128)S(1)} %get-tuple-element.37), channel_id=1, source_target_pairs={{0,16},{4,20},{8,24},{12,28},{16,0},{20,4},{24,8},{28,12},{1,17},{... | collective-permute-start | bytes 786440 | tf_op jit(solution)/shard_map/ppermute | solution.py:351
  84.0 13.3 %collective-permute-start.22 = (f32[4,128,128]{2,1,0:T(8,128)S(1)}, f32[4,128,128]{2,1,0:T(8,128)S(1)}, u32[]{:S(2)}, u32[]{:S(2)}) collective-permute-start(f32[4,128,128]{2,1,0:T(8,128)S(1)} %get-tuple-element.38), channel_id=1, source_target_pairs={{0,24},{4,28},{8,16},{12,20},{16,8},{20,12},{24,0},{28,4},{1,25},{... | collective-permute-start | bytes 786440 | tf_op jit(solution)/shard_map/ppermute | solution.py:351
  97.4 6.1 %collective-permute-start.23 = (f32[4,32,128]{2,1,0:T(8,128)S(1)}, f32[4,32,128]{2,1,0:T(8,128)S(1)}, u32[]{:S(2)}, u32[]{:S(2)}) collective-permute-start(f32[4,32,128]{2,1,0:T(8,128)S(1)} %get-tuple-element.41), channel_id=1, source_target_pairs={{0,3},{1,2},{2,1},{3,0},{4,7},{5,6},{6,5},{7,4},{8,11},{9,10},{10,... | collective-permute-start | bytes 196616 | tf_op jit(solution)/shard_map/ppermute | solution.py:351
  100.5 5.3 %collective-permute-start.24 = (f32[4,32,128]{2,1,0:T(8,128)S(1)}, f32[4,32,128]{2,1,0:T(8,128)S(1)}, u32[]{:S(2)}, u32[]{:S(2)}) collective-permute-start(f32[4,32,128]{2,1,0:T(8,128)S(1)} %get-tuple-element.43), channel_id=1, source_target_pairs={{0,2},{1,3},{2,0},{3,1},{4,6},{5,7},{6,4},{7,5},{8,10},{9,11},{10,... | collective-permute-start | bytes 196616 | tf_op jit(solution)/shard_map/ppermute | solution.py:351
  100.5 5.6 %collective-permute-start.25 = (f32[4,32,128]{2,1,0:T(8,128)S(1)}, f32[4,32,128]{2,1,0:T(8,128)S(1)}, u32[]{:S(2)}, u32[]{:S(2)}) collective-permute-start(f32[4,32,128]{2,1,0:T(8,128)S(1)} %get-tuple-element.42), channel_id=1, source_target_pairs={{0,1},{1,0},{2,3},{3,2},{4,5},{5,4},{6,7},{7,6},{8,9},{9,8},{10,11... | collective-permute-start | bytes 196616 | tf_op jit(solution)/shard_map/ppermute | solution.py:351
